TPU v7x, 256 devices: a whole 4x4x8 slice. The times are simulated.
256 devices in a mesh: gx: 8 (over y, core), gy: 32 (over z, x).
Axes of the slice: x: 4, y: 4, z: 8, core: 2. Of those that a mesh axis runs over, the one named last changes fastest.
Arguments:
- pressure: float32 [512, 512, 512], P('gx', 'gy'), may hold values from -6 to 6
- divergence: float32 [512, 512, 512], P('gx', 'gy'), may hold values from -6 to 6
- diagonal: float32 [512, 512, 512], P('gx', 'gy'), may hold values from 0.05 to 0.5
- normals: float32 [3, 262144], P(None, ('gx', 'gy')), may hold values from -6 to 6
- traction: float32 [3, 262144], P(None, ('gx', 'gy')), may hold values from -3 to 3
- slot_of: int32 [8, 32768], P('gx'), may hold values from 0 to 98303, as said below
- counts: int32 [256], P(('gx', 'gy')), may hold values from 0 to 3072, as said below
- previous: float32 [3, 786432], P(None, ('gx', 'gy')), may hold values from -6 to 6
- secant_v: float32 [32, 3, 786432], P(None, None, ('gx', 'gy')), may hold values from -6 to 6
- secant_w: float32 [32, 3, 786432], P(None, None, ('gx', 'gy')), may hold values from -940.60406 to 940.60406
Outputs:
- pressure_new: float32 [512, 512, 512], P('gx', 'gy')
- coupled: float32 [3, 786432], P(None, ('gx', 'gy'))
Inputs may be any that keep to these rules, and one draw needn't show every extreme that they name: Within each group (row of slot_of) the places are distinct; place o * 3072 + s has s < counts[a * 32 + o]; every such place is used; the rows of one device (aligned blocks of 1024 entries) send at most 96 rows to one owner, and exactly 96 to some owner. The counts of one group sum to 32768; some owner of every group holds exactly 3072.
All inputs are finite; a program needn't handle non-finite values.
Results may differ from a plain program's by a relative error of at most 0.00019.
Values sent between devices are 32-bit elements; how exact they have to be, the bound alone decides.
A program may use at most 128 MiB of HBM per device.

v0:
```python
import jax
import jax.numpy as jnp
from jax import lax
from jax.sharding import PartitionSpec as P

SWEEPS = 2


def extended(cells, sides, width):
    for axis, dim in sides:
        count = lax.axis_size(axis)
        ends = count - 1
        head = lax.slice_in_dim(cells, 0, width, axis=dim)
        tail = lax.slice_in_dim(cells, cells.shape[dim] - width, cells.shape[dim], axis=dim)
        cells = jnp.concatenate(
            [
                lax.ppermute(tail, axis, [(i, (i + 1) % count) for i in range(ends)]),
                cells,
                lax.ppermute(head, axis, [((i + 1) % count, i) for i in range(ends)]),
            ],
            axis=dim,
        )
    return cells


def stencil_sum(padded):
    padded = jnp.pad(padded, ((0, 0), (0, 0), (1, 1)))
    total = padded[2:, 1:-1, 1:-1] + padded[:-2, 1:-1, 1:-1]
    total = total + padded[1:-1, 2:, 1:-1] + padded[1:-1, :-2, 1:-1]
    total = total + padded[1:-1, 1:-1, 2:] + padded[1:-1, 1:-1, :-2]
    return total


def sweep_once(field, divergence, diagonal):
    padded = extended(field, (("gx", 0), ("gy", 1)), 1)
    return (divergence + stencil_sum(padded)) / (6.0 + diagonal)


def shards(
    pressure, divergence, diagonal, normals, traction, slot_of, counts, previous, secant_v, secant_w
):
    columns = secant_v.shape[0]
    capacity = previous.shape[1]
    slot_index = jnp.arange(capacity, dtype=jnp.int32)
    occupied = (slot_index < counts[0]).astype(jnp.float32)
    masked_v = (secant_v * occupied[None, None, :]).reshape(columns, 3 * capacity)
    gram_local = jnp.dot(masked_v, masked_v.T, precision=lax.Precision.HIGHEST)
    field = pressure
    for sweep_index in range(SWEEPS):
        field = sweep_once(field, divergence, diagonal)
    surface = field[:, :, -1].reshape(-1)
    forces = normals * surface[None, :] + traction
    own_index = lax.axis_index("gy")
    all_slots = slot_of[0]
    gathered = lax.all_gather(forces, "gy", axis=1, tiled=True)
    placed = jnp.where(all_slots // capacity == own_index, all_slots % capacity, capacity)
    owned = jnp.zeros((3, capacity), jnp.float32).at[:, placed].set(gathered, mode="drop")
    residual = occupied[None, :] * (owned - previous)
    projection_local = jnp.dot(
        masked_v, residual.reshape(3 * capacity), precision=lax.Precision.HIGHEST
    )
    gram, projection = lax.psum((gram_local, projection_local), ("gx", "gy"))
    factor = jnp.linalg.cholesky(gram)
    coefficient = -jax.scipy.linalg.cho_solve((factor, True), projection)
    update = jnp.dot(
        coefficient, secant_w.reshape(columns, 3 * capacity), precision=lax.Precision.HIGHEST
    ).reshape(3, capacity)
    coupled = occupied[None, :] * (owned + update)
    return (field, coupled)


def solution(mesh):
    placed = (
        P("gx", "gy", None),
        P("gx", "gy", None),
        P("gx", "gy", None),
        P(None, ("gx", "gy")),
        P(None, ("gx", "gy")),
        P("gx", None),
        P(("gx", "gy")),
        P(None, ("gx", "gy")),
        P(None, None, ("gx", "gy")),
        P(None, None, ("gx", "gy")),
    )
    return jax.shard_map(
        shards,
        mesh=mesh,
        in_specs=placed,
        out_specs=(P("gx", "gy", None), P(None, ("gx", "gy"))),
        check_vma=False,
    )
```

profile of v0, /device:TPU:1, one launch (start us, length us, event | category | flops | bytes accessed | tf_op | source)
XLA Modules:
  0.0 306.0 jit_solution(7569810159518206231)
XLA Ops:
  0.6 0.0 copy-start
  0.6 0.9 fusion.35
  1.6 5.1 %collective-permute-start = (f32[1,16,512]{2,0,1:T(1,128)S(1)}, f32[1,16,512]{2,0,1:T(1,128)S(1)}, u32[]{:S(2)}, u32[]{:S(2)}) collective-permute-start(f32[1,16,512]{2,0,1:T(1,128)S(1)} %copy.23), channel_id=1, source_target_pairs={{32,0},{64,32},{96,64},{128,96},{160,128},{192,160},{224,192},{33,... | collective-permute-start | bytes 98312 | tf_op jit(solution)/shard_map/ppermute | solution.py:19
  6.7 1.9 collective-permute-start.1
  8.6 2.8 copy.24
  11.5 0.0 copy-start.1
  11.5 0.0 copy-start.7
  11.5 0.0 collective-permute-done
  11.5 0.0 collective-permute-done.1
  11.6 1.4 collective-permute-start.2
  13.0 4.0 %collective-permute-start.3 = (f32[66,1,512]{2,0,1:T(8,128)S(1)}, f32[66,1,512]{2,0,1:T(8,128)S(1)}, u32[]{:S(2)}, u32[]{:S(2)}) collective-permute-start(f32[66,1,512]{2,0,1:T(8,128)S(1)} %get-tuple-element.12), channel_id=1, source_target_pairs={{0,1},{1,2},{2,3},{3,4},{4,5},{5,6},{6,7},{7,8},{8,9},{9,10},{10,1... | collective-permute-start | bytes 405512 | tf_op jit(solution)/shard_map/ppermute | solution.py:17
  17.0 0.0 copy-done.7
  17.0 1.8 compare_select_fusion
  19.4 0.0 copy-start.2
  19.5 0.0 copy-start.4
  19.5 0.0 collective-permute-done.2
  19.5 0.0 collective-permute-done.3
  19.5 0.0 copy-done.1
  19.5 2.8 select_maximum_fusion.4
  22.3 0.0 copy-done.2
  22.4 0.0 copy-done.4
  22.4 0.0 copy-start.8
  22.4 6.9 %fusion.7 = f32[64,16,512]{2,0,1:T(8,128)S(1)} fusion(f32[66,18,514]{2,0,1:T(8,128)S(1)} %select_maximum_fusion.4, f32[66,1,512]{2,0,1:T(8,128)S(1)} %collective-permute-done.3, f32[1,16,512]{2,0,1:T(1,128)S(1)} %collective-permute-done, f32[64,16,512]{2,0,1:T(8,128)} %copy-done.1, f32[1,16,512]{2,0,1:T(1,128)S(1)} %collective-permute-done.1, ...), kind=kLoop, calls=%fused_computation.29 | loop fusion | flops 8388608 | bytes 12918784 | tf_op jit(solution)/shard_map/div | solution.py:36
  29.3 0.1 fusion.34
  29.3 3.4 %collective-permute-start.4 = (f32[1,16,512]{2,0,1:T(1,128)S(1)}, f32[1,16,512]{2,0,1:T(1,128)S(1)}, u32[]{:S(2)}, u32[]{:S(2)}) collective-permute-start(f32[1,16,512]{2,0,1:T(1,128)S(1)} %get-tuple-element.15), channel_id=1, source_target_pairs={{32,0},{64,32},{96,64},{128,96},{160,128},{192,160},{224,192},{33,... | collective-permute-start | bytes 98312 | tf_op jit(solution)/shard_map/ppermute | solution.py:19
  32.8 2.6 collective-permute-start.5
  35.4 0.0 copy-done.8
  35.4 1.7 copy.35
  37.0 0.0 collective-permute-done.4
  37.1 0.0 collective-permute-done.5
  37.1 1.4 collective-permute-start.6
  38.5 4.9 %collective-permute-start.7 = (f32[66,1,512]{2,0,1:T(8,128)S(1)}, f32[66,1,512]{2,0,1:T(8,128)S(1)}, u32[]{:S(2)}, u32[]{:S(2)}) collective-permute-start(f32[66,1,512]{2,0,1:T(8,128)S(1)} %get-tuple-element.10), channel_id=1, source_target_pairs={{0,1},{1,2},{2,3},{3,4},{4,5},{5,6},{6,7},{7,8},{8,9},{9,10},{10,1... | collective-permute-start | bytes 405512 | tf_op jit(solution)/shard_map/ppermute | solution.py:17
  43.5 1.1 convolution_bitcast_fusion
  44.5 0.0 copy-start.3
  44.6 0.0 copy-start.5
  44.6 1.1 collective-permute-done.6
  45.7 0.9 collective-permute-done.7
  46.6 2.8 select_maximum_fusion
  49.5 6.7 %fusion.2 = f32[64,16,512]{2,0,1:T(8,128)S(1)} fusion(f32[66,18,514]{2,0,1:T(8,128)S(1)} %select_maximum_fusion, f32[66,1,512]{2,0,1:T(8,128)S(1)} %collective-permute-done.7, f32[1,16,512]{2,0,1:T(1,128)S(1)} %collective-permute-done.4, f32[64,16,512]{2,0,1:T(8,128)S(1)} %fusion.7, f32[1,16,512]{2,0,1:T(1,128)S(1)} %collective-permute-done.5, ...), kind=kLoop, calls=%fused_computation.14 | loop fusion | flops 8388608 | bytes 12918784 | tf_op jit(solution)/shard_map/div | solution.py:36
  56.2 0.2 slice.128
  56.4 0.0 copy-start.9
  56.4 0.0 copy-start.10
  56.4 2.5 copy.37
  59.0 0.5 copy.31
  59.5 0.1 mul.33
  59.5 0.0 copy-done.10
  59.6 48.0 %all_gather.3 = f32[3,32768]{1,0:T(4,128)S(1)} all-gather(f32[3,1024]{1,0:T(4,128)S(1)} %multiply_add_fusion), channel_id=1, replica_groups=mesh['gx'=8,'gy'=32] {'gy'}, dimensions={1}, use_global_device_ids=true | all-gather | bytes 405504 | tf_op jit(solution)/shard_map/all_gather | solution.py:55
  107.6 8.5 %copy.32 = f32[32768,3]{1,0:T(8,128)} copy(f32[32768,3]{0,1:T(4,128)S(1)} %bitcast.77) | data formatting | bytes 786432 | tf_op jit(solution)/shard_map/all_gather | solution.py:55
  116.1 80.8 %scatter_custom_fusion = f32[3,3072]{0,1:T(8,128)S(1)} fusion(s32[32768]{0:T(1024)} %bitcast.78, f32[32768,3]{1,0:T(8,128)} %copy.32, f32[]{:T(128)} %constant.70.clone.1), kind=kCustom, calls=%fused_computation.58 | custom fusion | bytes 37376 | tf_op jit(solution)/shard_map/scatter | solution.py:57
  196.9 3.0 multiply_bitcast_fusion
  200.0 1.9 copy.40
  201.8 2.3 fusion.20
  204.1 86.8 %all-reduce.2 = (f32[32,32]{0,1:T(8,128)S(1)}, f32[32]{0:T(128)S(1)}) all-reduce(f32[32,32]{0,1:T(8,128)S(1)} %convolution_bitcast_fusion, f32[32]{0:T(128)S(1)} %fusion.20), channel_id=1, replica_groups=mesh['gx'=8,'gy'=32] {'gx','gy'}, use_global_device_ids=true, to_apply=%region_1.2 | all-reduce | flops 1056 | bytes 8448 | tf_op jit(solution)/shard_map/psum | solution.py:62
  291.0 0.1 copy.34
  291.1 2.9 cholesky.16
  294.0 0.6 compare_reduce_fusion
  294.7 0.7 fusion.28
  295.3 2.4 custom-call.10
  297.7 0.2 convolution_bitcast_fusion.2
  297.9 0.1 fusion.19
  298.1 0.7 fusion.12
  298.7 1.7 copy.42
  300.4 3.0 fusion.11
  303.5 2.5 copy.38
  (14 shorter events, 0.2 us)
Async XLA Ops:
  0.6 297.4 %copy-start = (f32[32,3,3072]{2,0,1:T(8,128)S(1)}, f32[32,3,3072]{2,0,1:T(8,128)}, u32[]{:S(2)}) copy-start(f32[32,3,3072]{2,0,1:T(8,128)} %param.19) | copy-start | bytes 3538948
  1.6 9.9 %collective-permute-start = (f32[1,16,512]{2,0,1:T(1,128)S(1)}, f32[1,16,512]{2,0,1:T(1,128)S(1)}, u32[]{:S(2)}, u32[]{:S(2)}) collective-permute-start(f32[1,16,512]{2,0,1:T(1,128)S(1)} %copy.23), channel_id=1, source_target_pairs={{32,0},{64,32},{96,64},{128,96},{160,128},{192,160},{224,192},{33,... | collective-permute-start | bytes 98312 | tf_op jit(solution)/shard_map/ppermute | solution.py:19
  6.7 4.8 %collective-permute-start.1 = (f32[1,16,512]{2,0,1:T(1,128)S(1)}, f32[1,16,512]{2,0,1:T(1,128)S(1)}, u32[]{:S(2)}, u32[]{:S(2)}) collective-permute-start(f32[1,16,512]{2,0,1:T(1,128)S(1)} %copy.25), channel_id=1, source_target_pairs={{0,32},{32,64},{64,96},{96,128},{128,160},{160,192},{192,224},{1,3... | collective-permute-start | bytes 98312 | tf_op jit(solution)/shard_map/ppermute | solution.py:17
  11.5 8.0 %copy-start.1 = (f32[64,16,512]{2,0,1:T(8,128)}, f32[64,16,512]{2,0,1:T(8,128)S(1)}, u32[]{:S(2)}) copy-start(f32[64,16,512]{2,0,1:T(8,128)S(1)} %copy.24) | copy-start | bytes 6291460
  11.5 5.5 %copy-start.7 = (s32[1,32768]{1,0:T(1,128)S(1)}, s32[1,32768]{1,0:T(1,128)}, u32[]{:S(2)}) copy-start(s32[1,32768]{1,0:T(1,128)} %param.15) | copy-start | bytes 393220
  11.6 7.9 %collective-permute-start.2 = (f32[66,1,512]{2,0,1:T(8,128)S(1)}, f32[66,1,512]{2,0,1:T(8,128)S(1)}, u32[]{:S(2)}, u32[]{:S(2)}) collective-permute-start(f32[66,1,512]{2,0,1:T(8,128)S(1)} %get-tuple-element.13), channel_id=1, source_target_pairs={{1,0},{2,1},{3,2},{4,3},{5,4},{6,5},{7,6},{8,7},{9,8},{10,9},{11,1... | collective-permute-start | bytes 405512 | tf_op jit(solution)/shard_map/ppermute | solution.py:19
  13.0 6.5 %collective-permute-start.3 = (f32[66,1,512]{2,0,1:T(8,128)S(1)}, f32[66,1,512]{2,0,1:T(8,128)S(1)}, u32[]{:S(2)}, u32[]{:S(2)}) collective-permute-start(f32[66,1,512]{2,0,1:T(8,128)S(1)} %get-tuple-element.12), channel_id=1, source_target_pairs={{0,1},{1,2},{2,3},{3,4},{4,5},{5,6},{6,7},{7,8},{8,9},{9,10},{10,1... | collective-permute-start | bytes 405512 | tf_op jit(solution)/shard_map/ppermute | solution.py:17
  19.4 2.9 copy-start.2
  19.5 2.9 copy-start.4
  22.4 13.0 %copy-start.8 = (f32[3,3072]{1,0:T(4,128)S(1)}, f32[3,3072]{1,0:T(4,128)}, u32[]{:S(2)}) copy-start(f32[3,3072]{1,0:T(4,128)} %param.17) | copy-start | bytes 110596
  29.3 7.7 %collective-permute-start.4 = (f32[1,16,512]{2,0,1:T(1,128)S(1)}, f32[1,16,512]{2,0,1:T(1,128)S(1)}, u32[]{:S(2)}, u32[]{:S(2)}) collective-permute-start(f32[1,16,512]{2,0,1:T(1,128)S(1)} %get-tuple-element.15), channel_id=1, source_target_pairs={{32,0},{64,32},{96,64},{128,96},{160,128},{192,160},{224,192},{33,... | collective-permute-start | bytes 98312 | tf_op jit(solution)/shard_map/ppermute | solution.py:19
  32.8 4.3 %collective-permute-start.5 = (f32[1,16,512]{2,0,1:T(1,128)S(1)}, f32[1,16,512]{2,0,1:T(1,128)S(1)}, u32[]{:S(2)}, u32[]{:S(2)}) collective-permute-start(f32[1,16,512]{2,0,1:T(1,128)S(1)} %get-tuple-element.14), channel_id=1, source_target_pairs={{0,32},{32,64},{64,96},{96,128},{128,160},{160,192},{192,224},{1,3... | collective-permute-start | bytes 98312 | tf_op jit(solution)/shard_map/ppermute | solution.py:17
  37.0 6.4 %copy-start.6 = (f32[32,3,3072]{2,0,1:T(8,128)S(1)}, f32[32,3,3072]{2,0,1:T(8,128)}, u32[]{:S(2)}) copy-start(f32[32,3,3072]{2,0,1:T(8,128)} %param.18) | copy-start | bytes 3538948
  37.1 8.6 %collective-permute-start.6 = (f32[66,1,512]{2,0,1:T(8,128)S(1)}, f32[66,1,512]{2,0,1:T(8,128)S(1)}, u32[]{:S(2)}, u32[]{:S(2)}) collective-permute-start(f32[66,1,512]{2,0,1:T(8,128)S(1)} %get-tuple-element.11), channel_id=1, source_target_pairs={{1,0},{2,1},{3,2},{4,3},{5,4},{6,5},{7,6},{8,7},{9,8},{10,9},{11,1... | collective-permute-start | bytes 405512 | tf_op jit(solution)/shard_map/ppermute | solution.py:19
  38.5 8.1 %collective-permute-start.7 = (f32[66,1,512]{2,0,1:T(8,128)S(1)}, f32[66,1,512]{2,0,1:T(8,128)S(1)}, u32[]{:S(2)}, u32[]{:S(2)}) collective-permute-start(f32[66,1,512]{2,0,1:T(8,128)S(1)} %get-tuple-element.10), channel_id=1, source_target_pairs={{0,1},{1,2},{2,3},{3,4},{4,5},{5,6},{6,7},{7,8},{8,9},{9,10},{10,1... | collective-permute-start | bytes 405512 | tf_op jit(solution)/shard_map/ppermute | solution.py:17
  44.5 4.9 %copy-start.3 = (f32[64,16,512]{2,1,0:T(8,128)S(1)}, f32[64,16,512]{2,1,0:T(8,128)}, u32[]{:S(2)}) copy-start(f32[64,16,512]{2,1,0:T(8,128)} %param.11) | copy-start | bytes 6291460
  44.6 4.9 %copy-start.5 = (f32[64,16,512]{2,1,0:T(8,128)S(1)}, f32[64,16,512]{2,1,0:T(8,128)}, u32[]{:S(2)}) copy-start(f32[64,16,512]{2,1,0:T(8,128)} %param.12) | copy-start | bytes 6291460
  56.4 3.1 %copy-start.9 = (f32[3,1024]{1,0:T(4,128)S(1)}, f32[3,1024]{1,0:T(4,128)}, u32[]{:S(2)}) copy-start(f32[3,1024]{1,0:T(4,128)} %param.14) | copy-start | bytes 36868
  56.4 3.1 %copy-start.10 = (f32[3,1024]{1,0:T(4,128)S(1)}, f32[3,1024]{1,0:T(4,128)}, u32[]{:S(2)}) copy-start(f32[3,1024]{1,0:T(4,128)} %param.13) | copy-start | bytes 36868
where the time goes:
time: 307 us; the launch traced here: 306 us
  blocking collectives  135 us (44%)
  local copies, waits for them, and re-layouts  104 us (34%)
  other arithmetic  33.9 us (11%)
  starting transfers between devices  24.8 us (8%)
  matrix products  4.35 us (1%)
    psum x1, blocking collectives, shards(): gram, projection = lax.psum((gram_local, projection_local), ('gx', 'gy'))  86.8 us
    scatter x1, local copies, waits for them, and re-layouts, shards(): jnp.zeros((3, capacity), jnp.float32).at[:, placed]  80.8 us
    all_gather x1, blocking collectives, shards(): gathered = lax.all_gather(forces, 'gy', axis=1, tiled=True)  48 us
    div x2, other arithmetic, sweep_once(): return (divergence + stencil_sum(padded)) / (6.0 + diagonal)  13.6 us
    ppermute x4, starting transfers between devices, extended(): lax.ppermute(tail, axis, [(i, (i + 1) % count) for i in range(ends)])  13.4 us
    ppermute x4, starting transfers between devices, extended(): lax.ppermute(head, axis, [((i + 1) % count, i) for i in range(ends)])  11.4 us
    unnamed x26, local copies, waits for them, and re-layouts  9.59 us
    all_gather x1, local copies, waits for them, and re-layouts, shards(): gathered = lax.all_gather(forces, 'gy', axis=1, tiled=True)  8.53 us
  transfers between devices with their start and end apart: 8, of which 2 were waited for; matrix products, arithmetic and copies ran while one was open for 2% of the time, Pallas kernels for 0%

commit v1 on v0

v1 whole, which is shorter than its diff:
```python
import functools

import jax
import jax.numpy as jnp
from jax import lax
from jax.experimental import pallas as pl
from jax.experimental.pallas import tpu as pltpu
from jax.sharding import PartitionSpec as P

MESH = pl.DeviceIdType.MESH
F32 = jnp.float32
BF16 = jnp.bfloat16
NT = (((1,), (1,)), ((), ()))


def nt_dot(a, b):
    return lax.dot_general(a, b, NT, preferred_element_type=F32)


def split3(x):
    hi = x.astype(BF16).astype(F32)
    rest = x - hi
    mid = rest.astype(BF16).astype(F32)
    return hi, mid, rest - mid


def kernel(
    ngx, ngy,
    p_hbm, d_hbm, g_hbm, n_hbm, t_hbm, slot_hbm, cnt_hbm, prev_hbm, v_hbm, w_hbm,
    out_p, out_c,
    pp, pq, dv, gd, ob, vv, ww, nrm, trc, slt, cnt, prv, outc,
    slab, num, ons, bt1, mh, bt2, amat, xs,
    fj, fi, fc, ssb, srb, fsb, frb, gsb, grb, hsb, hrb, psb, prb, qsb, qrb,
    in_sem, out_sem, fs_sem, fr_sem, hs_sem, hr_sem, as_sem, ar_sem,
):
    gx = lax.axis_index("gx")
    gy = lax.axis_index("gy")
    K = 32
    CAPR = 24

    def wrap(i, n):
        return lax.rem(i + n, n)

    bar = pltpu.get_barrier_semaphore()
    for d in range(1, ngy):
        pl.semaphore_signal(bar, inc=1, device_id=(gx, wrap(gy + d, ngy)), device_id_type=MESH)
    for d in range(1, ngx):
        pl.semaphore_signal(bar, inc=1, device_id=(wrap(gx + d, ngx), gy), device_id_type=MESH)
    for a in (-1, 1):
        for b in (-1, 1):
            pl.semaphore_signal(
                bar, inc=1, device_id=(wrap(gx + a, ngx), wrap(gy + b, ngy)), device_id_type=MESH
            )

    copies = []

    def load(src, dst):
        c = pltpu.make_async_copy(src, dst, in_sem.at[len(copies)])
        c.start()
        copies.append(c)
        return c

    c_slot = load(slot_hbm.at[:, pl.ds(pl.multiple_of(gy * 1024, 1024), 1024)], slt)
    c_cnt = load(cnt_hbm, cnt)

    def tile_loads(t):
        lanes = pl.ds(128 * t, 128)
        return (
            load(p_hbm.at[:, :, lanes], pp.at[t, pl.ds(1, 64), pl.ds(8, 16), :]),
            load(d_hbm.at[:, :, lanes], dv.at[t]),
            load(g_hbm.at[:, :, lanes], gd.at[t]),
        )

    c_t3 = tile_loads(3)
    c_v = load(v_hbm, vv)
    c_n = load(n_hbm, nrm)
    c_t = load(t_hbm, trc)
    c_prev = load(prev_hbm, prv)
    c_rest = [c for t in range(3) for c in tile_loads(t)]
    c_w = load(w_hbm, ww)

    has_im, has_ip = gx > 0, gx < ngx - 1
    has_jm, has_jp = gy > 0, gy < ngy - 1

    def both(a, b):
        return jnp.logical_and(a, b)

    def zero_when(cond, ref):
        @pl.when(jnp.logical_not(cond))
        def _():
            ref[...] = jnp.zeros(ref.shape, ref.dtype)

    for f in (pp, pq):
        zero_when(has_im, f.at[:, 0:1, 8:24, :])
        zero_when(has_ip, f.at[:, 65:66, 8:24, :])
        zero_when(has_jm, f.at[:, 1:65, 7:8, :])
        zero_when(has_jp, f.at[:, 1:65, 24:25, :])
    zero_when(has_jm, fj.at[0])
    zero_when(has_jp, fj.at[1])
    zero_when(has_im, fi.at[0])
    zero_when(has_ip, fi.at[1])
    corner_has = (both(has_im, has_jm), both(has_im, has_jp), both(has_ip, has_jm), both(has_ip, has_jp))
    for k in range(4):
        zero_when(corner_has[k], fc.at[k])

    c_slot.wait()
    slot = slt[...].astype(F32)
    owner = jnp.floor((slot + 0.5) * (1.0 / 3072.0))
    place = slot - owner * 3072.0
    place_hi = jnp.floor((place + 0.5) * (1.0 / 256.0))
    place_lo = place - place_hi * 256.0
    oidx = lax.broadcasted_iota(jnp.int32, (32, 1024), 0).astype(F32)
    onehot = (oidx == owner).astype(F32)
    ons[...] = onehot
    upper = (
        lax.broadcasted_iota(jnp.int32, (128, 128), 0) > lax.broadcasted_iota(jnp.int32, (128, 128), 1)
    ).astype(BF16)
    ones = jnp.ones((128, 128), BF16)
    parts = [onehot[:, 128 * t : 128 * t + 128] for t in range(8)]
    stack = jnp.concatenate(parts, axis=0).astype(BF16)
    before = nt_dot(stack, upper)
    total = nt_dot(stack, ones)
    carry = jnp.zeros((32, 128), F32)
    ridx = lax.broadcasted_iota(jnp.int32, (128, 128), 0).astype(F32)
    for t in range(8):
        rank = jnp.sum(parts[t] * (before[32 * t : 32 * t + 32] + carry), axis=0, keepdims=True)
        carry = carry + total[32 * t : 32 * t + 32]
        bt1[:, 128 * t : 128 * t + 128] = (ridx == rank).astype(BF16)
    a2 = jnp.concatenate([onehot * place_hi, onehot * place_lo], axis=0).astype(BF16)
    sent = nt_dot(a2, bt1[...])
    ssb[0] = sent[:32]
    ssb[1] = sent[32:]
    srb[:, pl.ds(gy, 1), :] = ssb[:, pl.ds(gy, 1), :]

    for c in c_t3:
        c.wait()
    for t in range(8):
        lanes = slice(128 * t, 128 * t + 128)
        for k, x in enumerate(
            (
                pp[3, 1 + 8 * t : 9 + 8 * t, 8:24, :],
                dv[3, 8 * t : 8 * t + 8],
                gd[3, 8 * t : 8 * t + 8],
            )
        ):
            num[k, :, lanes] = x.reshape(128, 128).T[120:128]
    lane = lax.broadcasted_iota(jnp.int32, (8, 1024), 1)
    row = lax.broadcasted_iota(jnp.int32, (8, 1024), 0)
    jj = lane & 15
    P8 = num[0]
    D8 = num[1]
    R8 = 1.0 / (6.0 + num[2])

    def lateral(x):
        s = jnp.where(jj > 0, pltpu.roll(x, 1, 1), 0.0) + jnp.where(jj < 15, pltpu.roll(x, 1023, 1), 0.0)
        return s + jnp.where(lane >= 16, pltpu.roll(x, 16, 1), 0.0) + jnp.where(lane < 1008, pltpu.roll(x, 1008, 1), 0.0)

    N8 = D8 + pltpu.roll(P8, 1, 0) + jnp.where(row < 7, pltpu.roll(P8, 7, 0), 0.0) + lateral(P8)
    num[2] = R8
    num[3] = N8
    slab[...] = jnp.where(
        row >= 6, P8, jnp.where(row == 5, pltpu.roll(N8, 6, 0), pltpu.roll(R8, 5, 0))
    )

    c_cnt.wait()
    c_v.wait()
    count = cnt[0]
    gram = jnp.zeros((96, 128), F32)
    for c in range(3):
        for q in range(6):
            lo = 512 * q
            keep = lax.broadcasted_iota(jnp.int32, (K, 512), 1) + lo < count
            x = jnp.where(keep, vv[c, :, lo : lo + 512], 0.0)
            hi, mid, low = split3(x)
            s = jnp.concatenate([hi, mid, low, jnp.zeros_like(hi)], axis=0).astype(BF16)
            gram = gram + nt_dot(s[:96], s)
    gram = gram[0:32] + gram[32:64] + gram[64:96]
    gram = gram + pltpu.roll(gram, 96, 1) + pltpu.roll(gram, 64, 1)
    lane32 = lax.broadcasted_iota(jnp.int32, (32, 128), 1)
    gram = jnp.where(lane32 < 32, gram, 0.0)
    packed = gram[0:8]
    for t in range(1, 4):
        packed = packed + pltpu.roll(gram[8 * t : 8 * t + 8], 32 * t, 1)
    gsb[...] = packed
    grb[pl.ds(gy, 1)] = packed[None]

    pl.semaphore_wait(bar, (ngy - 1) + (ngx - 1) + 4)

    def remote(src, dst, ss, rs, dev):
        return pltpu.make_async_remote_copy(
            src_ref=src, dst_ref=dst, send_sem=ss, recv_sem=rs, device_id=dev, device_id_type=MESH
        )

    jm, jp = (gx, gy - 1), (gx, gy + 1)
    im, ip = (gx - 1, gy), (gx + 1, gy)
    lo_t, hi_t = pl.ds(0, 128), pl.ds(896, 128)
    faces = [
        (has_jm, jm, slab, fj.at[1], 1, 0),
        (has_jp, jp, slab, fj.at[0], 0, 1),
        (has_im, im, slab.at[:, lo_t], fi.at[1], 3, 2),
        (has_ip, ip, slab.at[:, hi_t], fi.at[0], 2, 3),
        (corner_has[0], (gx - 1, gy - 1), slab.at[:, lo_t], fc.at[3], 7, 4),
        (corner_has[1], (gx - 1, gy + 1), slab.at[:, lo_t], fc.at[2], 6, 5),
        (corner_has[2], (gx + 1, gy - 1), slab.at[:, hi_t], fc.at[1], 5, 6),
        (corner_has[3], (gx + 1, gy + 1), slab.at[:, hi_t], fc.at[0], 4, 7),
    ]
    face_dst = [fj.at[0], fj.at[1], fi.at[0], fi.at[1], fc.at[0], fc.at[1], fc.at[2], fc.at[3]]
    for cond, dev, src, dst, there, here in faces:
        @pl.when(cond)
        def _(dev=dev, src=src, dst=dst, there=there, here=here):
            remote(src, dst, fs_sem.at[here], fr_sem.at[there], dev).start()

    def to_group(src_of, dst, ss, rs):
        for d in range(1, ngy):
            o = wrap(gy + d, ngy)
            remote(src_of(o), dst, ss, rs, (gx, o)).start()

    def to_line(src, dst, ss, rs):
        for d in range(1, ngx):
            remote(src, dst, ss, rs, (wrap(gx + d, ngx), gy)).start()

    def wait_bytes(ref, sem):
        pltpu.make_async_copy(ref, ref, sem).wait()

    to_group(lambda o: ssb.at[:, pl.ds(o, 1), :], srb.at[:, pl.ds(gy, 1), :], as_sem.at[0], ar_sem.at[0])

    def halos(f, base):
        return [
            (has_jm, jm, f.at[:, 1:65, 8:9, :], f.at[:, 1:65, 24:25, :], base + 1, base + 0),
            (has_jp, jp, f.at[:, 1:65, 23:24, :], f.at[:, 1:65, 7:8, :], base + 0, base + 1),
            (has_im, im, f.at[:, 1:2, 8:24, :], f.at[:, 65:66, 8:24, :], base + 3, base + 2),
            (has_ip, ip, f.at[:, 64:65, 8:24, :], f.at[:, 0:1, 8:24, :], base + 2, base + 3),
        ]

    def send_halos(f, base):
        for cond, dev, src, dst, there, here in halos(f, base):
            @pl.when(cond)
            def _(dev=dev, src=src, dst=dst, there=there, here=here):
                remote(src, dst, hs_sem.at[here], hr_sem.at[there], dev).start()

    def wait_halos(f, base):
        into = (f.at[:, 1:65, 7:8, :], f.at[:, 1:65, 24:25, :], f.at[:, 0:1, 8:24, :], f.at[:, 65:66, 8:24, :])
        for (cond, dev, src, dst, there, here), mine in zip(halos(f, base), into):
            @pl.when(cond)
            def _(dev=dev, src=src, mine=mine, here=here):
                remote(src, mine, hs_sem.at[here], hr_sem.at[here], dev).wait_recv()

    def wait_halos_sent(f, base):
        for cond, dev, src, dst, there, here in halos(f, base):
            @pl.when(cond)
            def _(dev=dev, src=src, dst=dst, there=there, here=here):
                remote(src, dst, hs_sem.at[here], hr_sem.at[here], dev).wait_send()

    for c in c_rest:
        c.wait()
    send_halos(pp, 0)
    to_group(lambda o: gsb, grb.at[gy], as_sem.at[1], ar_sem.at[1])

    for (cond, dev, src, dst, there, here), mine in zip(faces, face_dst):
        @pl.when(cond)
        def _(dev=dev, src=src, mine=mine, here=here):
            remote(src, mine, fs_sem.at[here], fr_sem.at[here], dev).wait_recv()
    a_jm = jnp.where(jj == 0, pltpu.roll(fj[0], 1009, 1), 0.0)
    a_jp = jnp.where(jj == 15, pltpu.roll(fj[1], 15, 1), 0.0)
    lane1 = lax.broadcasted_iota(jnp.int32, (8, 128), 1)
    gap = jnp.zeros((8, 768), F32)
    a_i = jnp.concatenate(
        [
            jnp.where(lane1 < 16, pltpu.roll(fi[0], 16, 1), 0.0),
            gap,
            jnp.where(lane1 >= 112, pltpu.roll(fi[1], 112, 1), 0.0),
        ],
        axis=1,
    )
    corner = jnp.concatenate(
        [
            jnp.where(lane1 == 0, pltpu.roll(fc[0], 1, 1), 0.0)
            + jnp.where(lane1 == 15, pltpu.roll(fc[1], 31, 1), 0.0),
            gap,
            jnp.where(lane1 == 112, pltpu.roll(fc[2], 97, 1), 0.0)
            + jnp.where(lane1 == 127, pltpu.roll(fc[3], 127, 1), 0.0),
        ],
        axis=1,
    )
    P8 = num[0]
    D8 = num[1]
    R8 = num[2]
    once = (num[3] + a_jm + a_jp + a_i) * R8
    base = P8[7:8] + corner[7:8]
    beyond = (
        (a_jm[5:6] + base) * a_jm[4:5] + (a_jp[5:6] + base) * a_jp[4:5] + (a_i[5:6] + base) * a_i[4:5]
    )
    surface = (D8[7:8] + once[6:7] + lateral(once)[7:8] + beyond) * R8[7:8]
    c_n.wait()
    c_t.wait()
    forces = nrm[...] * surface + trc[...]

    onehot = ons[...]
    rows = []
    for piece in split3(forces):
        for c in range(3):
            rows.append((onehot * piece[c : c + 1]).astype(BF16))
    moved = nt_dot(jnp.concatenate(rows, axis=0), bt1[...])
    moved = moved[0:96] + moved[96:192] + moved[192:288]
    for c in range(3):
        fsb[c] = moved[32 * c : 32 * c + 32]
    frb[:, pl.ds(gy, 1), :] = fsb[:, pl.ds(gy, 1), :]
    to_group(lambda o: fsb.at[:, pl.ds(o, 1), :], frb.at[:, pl.ds(gy, 1), :], as_sem.at[2], ar_sem.at[2])

    lane2 = lax.broadcasted_iota(jnp.int32, (16, 128), 1)

    def plane_sum(f, i):
        xs_ = [f[t, i + 1, 8:24, :] for t in range(4)]
        rr = [pltpu.roll(x, 1, 1) for x in xs_]
        rl = [pltpu.roll(x, 127, 1) for x in xs_]
        zero = jnp.zeros((16, 128), F32)
        res = []
        for t in range(4):
            down = jnp.where(lane2 == 0, rr[t - 1] if t > 0 else zero, rr[t])
            up = jnp.where(lane2 == 127, rl[t + 1] if t < 3 else zero, rl[t])
            s = f[t, i, 8:24, :] + f[t, i + 2, 8:24, :]
            s = s + (f[t, i + 1, 7:23, :] + f[t, i + 1, 9:25, :])
            res.append(dv[t, i] + s + (up + down))
        return res

    wait_halos(pp, 0)

    def sweep1(i, carry):
        sums = plane_sum(pp, i)
        for t in range(4):
            r = 1.0 / (6.0 + gd[t, i])
            gd[t, i] = r
            pq[t, i + 1, 8:24, :] = sums[t] * r
        return carry

    lax.fori_loop(0, 64, sweep1, 0, unroll=2)
    send_halos(pq, 4)

    wait_bytes(srb.at[:, pl.ds(0, ngy - 1), :], ar_sem.at[0])
    hidx = lax.broadcasted_iota(jnp.int32, (16, 128), 0).astype(F32)
    lidx = lax.broadcasted_iota(jnp.int32, (256, 128), 0).astype(F32)
    for b in range(ngy):
        lanes = slice(128 * b, 128 * b + 128)
        mh[:, lanes] = (hidx == srb[0, b : b + 1, :]).astype(F32)
        bt2[:, lanes] = (lidx == srb[1, b : b + 1, :]).astype(BF16)

    wait_bytes(grb.at[pl.ds(0, ngy - 1)], ar_sem.at[1])
    packed = jnp.sum(grb[...], axis=0)
    hsb[...] = packed
    hrb[pl.ds(gx, 1)] = packed[None]
    to_line(hsb, hrb.at[gx], as_sem.at[3], ar_sem.at[3])

    wait_bytes(frb.at[:, pl.ds(0, ngy - 1), :], ar_sem.at[2])
    for c in range(3):
        pieces = split3(frb[c])
        for b in range(ngy):
            lanes = slice(128 * b, 128 * b + 128)
            m = mh[:, lanes]
            for s in range(3):
                r0 = 48 * s + 16 * c
                amat[r0 : r0 + 16, lanes] = (m * pieces[s][b : b + 1]).astype(BF16)
    own = nt_dot(amat[...], bt2[...])
    xs[...] = own[0:48] + own[48:96] + own[96:144]
    c_prev.wait()

    def slot_row(ref, c, h):
        return ref[16 * c + h // 2 : 16 * c + h // 2 + 1, 128 * (h % 2) : 128 * (h % 2) + 128]

    lane_row = lax.broadcasted_iota(jnp.int32, (1, 128), 1)
    acc = [jnp.zeros((8, 128), F32) for _ in range(4)]
    for h in range(CAPR):
        keep = lane_row + 128 * h < count
        lanes = slice(128 * h, 128 * h + 128)
        for c in range(3):
            res = jnp.where(keep, slot_row(xs, c, h) - prv[c : c + 1, lanes], 0.0)
            for k in range(4):
                acc[k] = acc[k] + vv[c, 8 * k : 8 * k + 8, lanes] * res
    diag = lax.broadcasted_iota(jnp.int32, (32, 128), 0) == lane32

    def to_row(col):
        return jnp.sum(jnp.where(diag, col, 0.0), axis=0, keepdims=True)

    def to_col(r):
        return jnp.sum(jnp.where(diag, r, 0.0), axis=1, keepdims=True)

    prow = to_row(jnp.sum(jnp.concatenate(acc, axis=0), axis=1, keepdims=True))
    psb[...] = prow
    prb[pl.ds(gy, 1), :] = prow
    to_group(lambda o: psb, prb.at[pl.ds(gy, 1), :], as_sem.at[4], ar_sem.at[4])

    wait_halos(pq, 4)

    def sweep2(i, carry):
        sums = plane_sum(pq, i)
        for t in range(4):
            ob[t, i] = sums[t] * gd[t, i]
        return carry

    c_out = []
    for q in range(4):
        lax.fori_loop(16 * q, 16 * q + 16, sweep2, 0, unroll=2)
        for t in range(4):
            c = pltpu.make_async_copy(
                ob.at[t, pl.ds(16 * q, 16)],
                out_p.at[pl.ds(16 * q, 16), :, pl.ds(128 * t, 128)],
                out_sem.at[4 * q + t],
            )
            c.start()
            c_out.append(c)

    wait_bytes(hrb.at[pl.ds(0, ngx - 1)], ar_sem.at[3])
    packed = jnp.sum(hrb[...], axis=0)
    m = jnp.concatenate([packed] + [pltpu.roll(packed, 128 - 32 * t, 1) for t in range(1, 4)], axis=0)
    sub32 = lax.broadcasted_iota(jnp.int32, (32, 128), 0)
    m = jnp.where(lane32 < 32, m, (sub32 + 32 == lane32).astype(F32))
    dinv = jnp.zeros((32, 1), F32)
    sub1 = lax.broadcasted_iota(jnp.int32, (32, 1), 0)
    for k in range(K):
        r = m[k : k + 1]
        inv = 1.0 / r[:, k : k + 1]
        dinv = jnp.where(sub1 == k, inv, dinv)
        if k < K - 1:
            f = jnp.where(sub1 > k, m[:, k : k + 1] * inv, 0.0)
            m = m - f * r
    linv = jnp.where(lane32 < 32, pltpu.roll(m, 96, 1), 0.0)

    wait_bytes(prb.at[pl.ds(0, ngy - 1), :], ar_sem.at[4])
    prow = jnp.sum(prb[...], axis=0, keepdims=True)
    qsb[...] = prow
    qrb[pl.ds(gx, 1), :] = prow
    to_line(qsb, qrb.at[pl.ds(gx, 1), :], as_sem.at[5], ar_sem.at[5])
    c_w.wait()
    wait_bytes(qrb.at[pl.ds(0, ngx - 1), :], ar_sem.at[5])
    prow = jnp.sum(qrb[...], axis=0, keepdims=True)
    y = jnp.sum(linv * prow, axis=1, keepdims=True) * dinv
    coef = to_col(-jnp.sum(linv * y, axis=0, keepdims=True))
    cb = [jnp.broadcast_to(coef[8 * k : 8 * k + 8], (8, 128)) for k in range(4)]
    for h in range(CAPR):
        keep = lane_row + 128 * h < count
        lanes = slice(128 * h, 128 * h + 128)
        for c in range(3):
            u = cb[0] * ww[c, 0:8, lanes] + cb[1] * ww[c, 8:16, lanes]
            u = u + (cb[2] * ww[c, 16:24, lanes] + cb[3] * ww[c, 24:32, lanes])
            u = jnp.sum(u, axis=0, keepdims=True)
            outc[c : c + 1, lanes] = jnp.where(keep, slot_row(xs, c, h) + u, 0.0)
    c = pltpu.make_async_copy(outc, out_c, out_sem.at[16])
    c.start()
    c_out.append(c)

    for cond, dev, src, dst, there, here in faces:
        @pl.when(cond)
        def _(dev=dev, src=src, dst=dst, here=here):
            remote(src, dst, fs_sem.at[here], fr_sem.at[here], dev).wait_send()
    wait_halos_sent(pp, 0)
    wait_halos_sent(pq, 4)
    wait_bytes(srb.at[:, pl.ds(0, ngy - 1), :], as_sem.at[0])
    wait_bytes(grb.at[pl.ds(0, ngy - 1)], as_sem.at[1])
    wait_bytes(frb.at[:, pl.ds(0, ngy - 1), :], as_sem.at[2])
    wait_bytes(hrb.at[pl.ds(0, ngx - 1)], as_sem.at[3])
    wait_bytes(prb.at[pl.ds(0, ngy - 1), :], as_sem.at[4])
    wait_bytes(qrb.at[pl.ds(0, ngx - 1), :], as_sem.at[5])
    for c in c_out:
        c.wait()


def shards(
    ngx, ngy,
    pressure, divergence, diagonal, normals, traction, slot_of, counts, previous, secant_v, secant_w,
):
    v = jnp.transpose(secant_v, (1, 0, 2))
    w = jnp.transpose(secant_w, (1, 0, 2))
    any_spec = pl.BlockSpec(memory_space=pl.ANY)
    vm = pltpu.VMEM
    dma = pltpu.SemaphoreType.DMA
    return pl.pallas_call(
        functools.partial(kernel, ngx, ngy),
        out_shape=(
            jax.ShapeDtypeStruct(pressure.shape, F32),
            jax.ShapeDtypeStruct(previous.shape, F32),
        ),
        in_specs=[any_spec] * 10,
        out_specs=(any_spec, any_spec),
        scratch_shapes=[
            vm((4, 66, 32, 128), F32),
            vm((4, 66, 32, 128), F32),
            vm((4, 64, 16, 128), F32),
            vm((4, 64, 16, 128), F32),
            vm((4, 64, 16, 128), F32),
            vm((3, 32, 3072), F32),
            vm((3, 32, 3072), F32),
            vm((3, 1024), F32),
            vm((3, 1024), F32),
            vm((1, 1024), jnp.int32),
            pltpu.SMEM((1,), jnp.int32),
            vm((3, 3072), F32),
            vm((3, 3072), F32),
            vm((8, 1024), F32),
            vm((4, 8, 1024), F32),
            vm((32, 1024), F32),
            vm((128, 1024), BF16),
            vm((16, 128 * ngy), F32),
            vm((256, 128 * ngy), BF16),
            vm((144, 128 * ngy), BF16),
            vm((48, 256), F32),
            vm((2, 8, 1024), F32),
            vm((2, 8, 128), F32),
            vm((4, 8, 128), F32),
            vm((2, 32, 128), F32),
            vm((2, 32, 128), F32),
            vm((3, 32, 128), F32),
            vm((3, 32, 128), F32),
            vm((8, 128), F32),
            vm((ngy, 8, 128), F32),
            vm((8, 128), F32),
            vm((ngx, 8, 128), F32),
            vm((1, 128), F32),
            vm((ngy, 128), F32),
            vm((1, 128), F32),
            vm((ngx, 128), F32),
            dma((24,)),
            dma((17,)),
            dma((8,)),
            dma((8,)),
            dma((8,)),
            dma((8,)),
            dma((6,)),
            dma((6,)),
        ],
        compiler_params=pltpu.CompilerParams(
            collective_id=0, has_side_effects=True, vmem_limit_bytes=48 * 1024 * 1024
        ),
    )(pressure, divergence, diagonal, normals, traction, slot_of, counts, previous, v, w)


def solution(mesh):
    placed = (
        P("gx", "gy", None),
        P("gx", "gy", None),
        P("gx", "gy", None),
        P(None, ("gx", "gy")),
        P(None, ("gx", "gy")),
        P("gx", None),
        P(("gx", "gy")),
        P(None, ("gx", "gy")),
        P(None, None, ("gx", "gy")),
        P(None, None, ("gx", "gy")),
    )
    return jax.shard_map(
        functools.partial(shards, mesh.shape["gx"], mesh.shape["gy"]),
        mesh=mesh,
        in_specs=placed,
        out_specs=(P("gx", "gy", None), P(None, ("gx", "gy"))),
        check_vma=False,
    )
```

time: 307 us -> 47.2 us (0.15)
  the two profiles are of different devices: /device:TPU:1 before, /device:TPU:32 now
where the time goes in v1:
time: 47.2 us; the launch traced here: 46.9 us
  Pallas kernels  38 us (81%)
  local copies, waits for them, and re-layouts  7.61 us (16%)
  between operations  1.3 us (3%)
    pallas_call x1, Pallas kernels, shards(): pl.pallas_call(functools.partial(kernel, ngx, ngy), out_shape=(jax.ShapeD...  38 us
    unnamed x14, local copies, waits for them, and re-layouts  7.61 us

profile of v1, /device:TPU:32, one launch (start us, length us, event | category | flops | bytes accessed | tf_op | source)
XLA Modules:
  0.0 46.9 jit_solution(9285756875851615148)
XLA Ops:
  1.3 0.0 copy-start
  1.3 1.3 %copy-done = f32[32,3,3072]{2,0,1:T(8,128)S(1)} copy-done((f32[32,3,3072]{2,0,1:T(8,128)S(1)}, f32[32,3,3072]{2,0,1:T(8,128)}, u32[]{:S(2)}) %copy-start) | copy-done | bytes 1179672
  2.5 0.0 copy-start.1
  2.6 1.3 %copy-done.1 = f32[32,3,3072]{2,0,1:T(8,128)S(1)} copy-done((f32[32,3,3072]{2,0,1:T(8,128)S(1)}, f32[32,3,3072]{2,0,1:T(8,128)}, u32[]{:S(2)}) %copy-start.1) | copy-done | bytes 1179672
  3.8 0.0 copy-start.2
  3.8 0.9 %copy-done.2 = s32[1,32768]{1,0:T(1,128)S(1)} copy-done((s32[1,32768]{1,0:T(1,128)S(1)}, s32[1,32768]{1,0:T(1,128)}, u32[]{:S(2)}) %copy-start.2) | copy-done | bytes 131096
  4.7 0.0 copy-start.3
  4.7 0.8 %copy-done.3 = f32[3,3072]{1,0:T(4,128)S(1)} copy-done((f32[3,3072]{1,0:T(4,128)S(1)}, f32[3,3072]{1,0:T(4,128)}, u32[]{:S(2)}) %copy-start.3) | copy-done | bytes 36888
  5.5 0.0 copy-start.4
  5.5 0.7 %copy-done.4 = f32[3,1024]{1,0:T(4,128)S(1)} copy-done((f32[3,1024]{1,0:T(4,128)S(1)}, f32[3,1024]{1,0:T(4,128)}, u32[]{:S(2)}) %copy-start.4) | copy-done | bytes 12312
  6.2 0.0 copy-start.5
  6.2 0.7 %copy-done.5 = f32[3,1024]{1,0:T(4,128)S(1)} copy-done((f32[3,1024]{1,0:T(4,128)S(1)}, f32[3,1024]{1,0:T(4,128)}, u32[]{:S(2)}) %copy-start.5) | copy-done | bytes 12312
  7.0 38.0 %shard_map.113 = (f32[64,16,512]{2,1,0:T(8,128)S(1)}, f32[3,3072]{1,0:T(4,128)S(1)}) custom-call(f32[64,16,512]{2,1,0:T(8,128)} %p_hbm.1, f32[64,16,512]{2,1,0:T(8,128)} %d_hbm.1, f32[64,16,512]{2,1,0:T(8,128)} %g_hbm.1, f32[3,1024]{1,0:T(4,128)S(1)} %copy-done.4, f32[3,1024]{1,0:T(4,128)S(1)} %copy-done.5, s32[1,32768]{1,0:T(1,128)S(1)} %copy-done.2, ...), custom_call_target="tpu_custom_call" | custom-call | tf_op jit(solution)/shard_map/pallas_call | solution.py:475
  44.9 1.3 %copy.15 = f32[64,16,512]{2,1,0:T(8,128)} copy(f32[64,16,512]{2,1,0:T(8,128)S(1)} %get-tuple-element.4) | data formatting | bytes 4194304
  46.3 0.6 %copy.16 = f32[3,3072]{1,0:T(4,128)} copy(f32[3,3072]{1,0:T(4,128)S(1)} %get-tuple-element.5) | data formatting | bytes 73728
Async XLA Ops:
  1.3 1.3 %copy-start = (f32[32,3,3072]{2,0,1:T(8,128)S(1)}, f32[32,3,3072]{2,0,1:T(8,128)}, u32[]{:S(2)}) copy-start(f32[32,3,3072]{2,0,1:T(8,128)} %param.18) | copy-start | bytes 3538948
  2.5 1.3 %copy-start.1 = (f32[32,3,3072]{2,0,1:T(8,128)S(1)}, f32[32,3,3072]{2,0,1:T(8,128)}, u32[]{:S(2)}) copy-start(f32[32,3,3072]{2,0,1:T(8,128)} %param.19) | copy-start | bytes 3538948
  3.8 0.9 %copy-start.2 = (s32[1,32768]{1,0:T(1,128)S(1)}, s32[1,32768]{1,0:T(1,128)}, u32[]{:S(2)}) copy-start(s32[1,32768]{1,0:T(1,128)} %slot_hbm.1) | copy-start | bytes 393220
  4.7 0.8 %copy-start.3 = (f32[3,3072]{1,0:T(4,128)S(1)}, f32[3,3072]{1,0:T(4,128)}, u32[]{:S(2)}) copy-start(f32[3,3072]{1,0:T(4,128)} %prev_hbm.1) | copy-start | bytes 110596
  5.5 0.7 %copy-start.4 = (f32[3,1024]{1,0:T(4,128)S(1)}, f32[3,1024]{1,0:T(4,128)}, u32[]{:S(2)}) copy-start(f32[3,1024]{1,0:T(4,128)} %n_hbm.1) | copy-start | bytes 36868
  6.2 0.7 %copy-start.5 = (f32[3,1024]{1,0:T(4,128)S(1)}, f32[3,1024]{1,0:T(4,128)}, u32[]{:S(2)}) copy-start(f32[3,1024]{1,0:T(4,128)} %t_hbm.1) | copy-start | bytes 36868

commit v2 on v1

v2 whole, which is shorter than its diff:
```python
import functools

import jax
import jax.numpy as jnp
from jax import lax
from jax.experimental import pallas as pl
from jax.experimental.pallas import tpu as pltpu
from jax.sharding import PartitionSpec as P

MESH = pl.DeviceIdType.MESH
F32 = jnp.float32
BF16 = jnp.bfloat16
NT = (((1,), (1,)), ((), ()))


def nt_dot(a, b):
    return lax.dot_general(a, b, NT, preferred_element_type=F32)


def split3(x):
    hi = x.astype(BF16).astype(F32)
    rest = x - hi
    mid = rest.astype(BF16).astype(F32)
    return hi, mid, rest - mid


def kernel(
    ngx, ngy,
    p_hbm, d_hbm, g_hbm, n_hbm, t_hbm, slot_hbm, cnt, prev_hbm, v_hbm, w_hbm,
    out_p, ww, xs, occ, cof,
    pp, pq, dv, gd, rv, vv, nrm, trc, slt, prv,
    slab, num, ons, bt1, mh, bt2, amat,
    fj, fi, fc, ssb, srb, fsb, frb, near, msk, acc0, gsb, gxb, gxs, grb, hsb, hrb, psb, prb, qsb, qrb,
    in_sem, fs_sem, fr_sem, hs_sem, hr_sem, as_sem, ar_sem, gr_sem, sl_sem, news,
):
    gx = lax.axis_index("gx")
    gy = lax.axis_index("gy")
    K = 32
    UNROLL = 4
    CAPR = 24

    NZ, NX = ngy // 4, 4
    OFF = sorted(
        ((dz, dx) for dz in range(NZ) for dx in range(NX)),
        key=lambda o: (min(o[0], NZ - o[0]) + min(o[1], NX - o[1]), o),
    )
    gz, gq = lax.div(gy, NX), lax.rem(gy, NX)

    def peer(off):
        return lax.rem(gz + off[0], NZ) * NX + lax.rem(gq + off[1], NX)

    def wrap(i, n):
        return lax.rem(i + n, n)

    copies = []

    def load(src, dst):
        c = pltpu.make_async_copy(src, dst, in_sem.at[len(copies)])
        c.start()
        copies.append(c)
        return c

    def lanes_of(t):
        return pl.ds(128 * t, 128)

    def load_p(t):
        return load(p_hbm.at[:, :, lanes_of(t)], pp.at[t, pl.ds(1, 64), pl.ds(8, 16), :])

    c_t3 = (
        load_p(3),
        load(d_hbm.at[:, :, lanes_of(3)], dv.at[3]),
        load(g_hbm.at[:, :, lanes_of(3)], gd.at[3]),
    )
    bar = pltpu.get_barrier_semaphore()
    greet = [
        (wrap(gx + a, ngx), wrap(gy + b, ngy)) for a in (-1, 0, 1) for b in (-1, 0, 1) if (a, b) != (0, 0)
    ]
    greet += [(gx, peer(o)) for o in ((1, 0), (NZ - 1, 0), (2, 0), (NZ - 2, 0), (0, 1), (0, 3), (0, 2))]
    greet += [(wrap(gx + a, ngx), gy) for a in range(2, ngx - 1)]
    for dev in greet:
        pl.semaphore_signal(bar, inc=1, device_id=dev, device_id_type=MESH)

    c_slot = load(slot_hbm.at[:, pl.ds(pl.multiple_of(gy * 1024, 1024), 1024)], slt)
    c_p = [load_p(t) for t in range(3)]
    c_n = load(n_hbm, nrm)
    c_t = load(t_hbm, trc)
    c_v = load(v_hbm, vv)
    c_dg = [load(d_hbm.at[:, :, lanes_of(t)], dv.at[t]) for t in range(3)]
    c_dg += [load(g_hbm.at[:, :, lanes_of(t)], gd.at[t]) for t in range(3)]
    c_prev = load(prev_hbm, prv)
    c_w = load(w_hbm, ww)

    has_im, has_ip = gx > 0, gx < ngx - 1
    has_jm, has_jp = gy > 0, gy < ngy - 1

    def both(a, b):
        return jnp.logical_and(a, b)

    def zero_when(cond, ref):
        @pl.when(jnp.logical_not(cond))
        def _():
            ref[...] = jnp.zeros(ref.shape, ref.dtype)

    for f in (pp, pq):
        zero_when(has_im, f.at[:, 0:1, 8:24, :])
        zero_when(has_ip, f.at[:, 65:66, 8:24, :])
        zero_when(has_jm, f.at[:, 1:65, 7:8, :])
        zero_when(has_jp, f.at[:, 1:65, 24:25, :])
    zero_when(has_jm, fj.at[0])
    zero_when(has_jp, fj.at[1])
    zero_when(has_im, fi.at[0])
    zero_when(has_ip, fi.at[1])
    corner_has = (both(has_im, has_jm), both(has_im, has_jp), both(has_ip, has_jm), both(has_ip, has_jp))
    for k in range(4):
        zero_when(corner_has[k], fc.at[k])

    def remote(src, dst, ss, rs, dev):
        return pltpu.make_async_remote_copy(
            src_ref=src, dst_ref=dst, send_sem=ss, recv_sem=rs, device_id=dev, device_id_type=MESH
        )

    jm, jp = (gx, gy - 1), (gx, gy + 1)
    im, ip = (gx - 1, gy), (gx + 1, gy)
    lo_t, hi_t = pl.ds(0, 128), pl.ds(896, 128)
    faces = [
        (has_jm, jm, slab.at[4:8], fj.at[1, 4:8], 1, 0),
        (has_jp, jp, slab.at[4:8], fj.at[0, 4:8], 0, 1),
        (has_im, im, slab.at[4:8, lo_t], fi.at[1, 4:8], 3, 2),
        (has_ip, ip, slab.at[4:8, hi_t], fi.at[0, 4:8], 2, 3),
        (corner_has[0], (gx - 1, gy - 1), slab.at[4:8, lo_t], fc.at[3, 4:8], 7, 4),
        (corner_has[1], (gx - 1, gy + 1), slab.at[4:8, lo_t], fc.at[2, 4:8], 6, 5),
        (corner_has[2], (gx + 1, gy - 1), slab.at[4:8, hi_t], fc.at[1, 4:8], 5, 6),
        (corner_has[3], (gx + 1, gy + 1), slab.at[4:8, hi_t], fc.at[0, 4:8], 4, 7),
    ]
    face_dst = [f.at[k, 4:8] for f, n in ((fj, 2), (fi, 2), (fc, 4)) for k in range(n)]
    def to_group(src_of, dst_of, ss, rs_of):
        for r in range(ngy - 1, 0, -1):
            o = peer(OFF[r])
            remote(src_of(o), dst_of(r), ss, rs_of(r), (gx, o)).start()

    def to_line(src, dst, ss, rs):
        for d in range(1, ngx):
            remote(src, dst, ss, rs, (wrap(gx + d, ngx), gy)).start()

    def wait_bytes(ref, sem):
        pltpu.make_async_copy(ref, ref, sem).wait()

    def halos(f, base):
        return [
            (has_jm, jm, f.at[:, 1:65, 8:9, :], f.at[:, 1:65, 24:25, :], base + 1, base + 0),
            (has_jp, jp, f.at[:, 1:65, 23:24, :], f.at[:, 1:65, 7:8, :], base + 0, base + 1),
            (has_im, im, f.at[:, 1:2, 8:24, :], f.at[:, 65:66, 8:24, :], base + 3, base + 2),
            (has_ip, ip, f.at[:, 64:65, 8:24, :], f.at[:, 0:1, 8:24, :], base + 2, base + 3),
        ]

    def send_halos(f, base):
        for cond, dev, src, dst, there, here in halos(f, base):
            @pl.when(cond)
            def _(dev=dev, src=src, dst=dst, there=there, here=here):
                remote(src, dst, hs_sem.at[here], hr_sem.at[there], dev).start()

    def wait_halos(f, base):
        into = (f.at[:, 1:65, 7:8, :], f.at[:, 1:65, 24:25, :], f.at[:, 0:1, 8:24, :], f.at[:, 65:66, 8:24, :])
        for (cond, dev, src, dst, there, here), mine in zip(halos(f, base), into):
            @pl.when(cond)
            def _(dev=dev, src=src, mine=mine, here=here):
                remote(src, mine, hs_sem.at[here], hr_sem.at[here], dev).wait_recv()

    def wait_halos_sent(f, base):
        for cond, dev, src, dst, there, here in halos(f, base):
            @pl.when(cond)
            def _(dev=dev, src=src, dst=dst, there=there, here=here):
                remote(src, dst, hs_sem.at[here], hr_sem.at[here], dev).wait_send()

    for k, c in enumerate(c_t3):
        c.wait()
        for t in range(8):
            x = pp[3, 1 + 8 * t : 9 + 8 * t, 8:24, :] if k == 0 else (dv, gd)[k - 1][3, 8 * t : 8 * t + 8]
            num[k, :, 128 * t : 128 * t + 128] = x.reshape(128, 128).T[120:128]
    lane = lax.broadcasted_iota(jnp.int32, (8, 1024), 1)
    row = lax.broadcasted_iota(jnp.int32, (8, 1024), 0)
    jj = lane & 15
    P8 = num[0]
    D8 = num[1]
    R8 = 1.0 / (6.0 + num[2])

    def lateral(x):
        s = jnp.where(jj > 0, pltpu.roll(x, 1, 1), 0.0) + jnp.where(jj < 15, pltpu.roll(x, 1023, 1), 0.0)
        return s + jnp.where(lane >= 16, pltpu.roll(x, 16, 1), 0.0) + jnp.where(lane < 1008, pltpu.roll(x, 1008, 1), 0.0)

    N8 = D8 + pltpu.roll(P8, 1, 0) + jnp.where(row < 7, pltpu.roll(P8, 7, 0), 0.0) + lateral(P8)
    num[2] = R8
    num[3] = N8
    slab[...] = jnp.where(
        row >= 6, P8, jnp.where(row == 5, pltpu.roll(N8, 6, 0), pltpu.roll(R8, 5, 0))
    )

    pl.semaphore_wait(bar, len(greet))

    for cond, dev, src, dst, there, here in faces:
        @pl.when(cond)
        def _(dev=dev, src=src, dst=dst, there=there, here=here):
            remote(src, dst, fs_sem.at[here], fr_sem.at[there], dev).start()

    for o in ((1, 0), (NZ - 1, 0), (2, 0), (NZ - 2, 0)):
        pl.semaphore_signal(news.at[0], inc=1, device_id=(gx, peer(o)), device_id_type=MESH)

    for c in c_p:
        c.wait()
    send_halos(pp, 0)

    c_slot.wait()
    slot = slt[...].astype(F32)
    owner = jnp.floor((slot + 0.5) * (1.0 / 3072.0))
    place = slot - owner * 3072.0
    place_hi = jnp.floor((place + 0.5) * (1.0 / 256.0))
    place_lo = place - place_hi * 256.0
    oidx = lax.broadcasted_iota(jnp.int32, (32, 1024), 0).astype(F32)
    onehot = (oidx == owner).astype(F32)
    ons[...] = onehot
    upper = (
        lax.broadcasted_iota(jnp.int32, (128, 128), 0) > lax.broadcasted_iota(jnp.int32, (128, 128), 1)
    ).astype(BF16)
    ones = jnp.ones((128, 128), BF16)
    parts = [onehot[:, 128 * t : 128 * t + 128] for t in range(8)]
    stack = jnp.concatenate(parts, axis=0).astype(BF16)
    before = nt_dot(stack, upper)
    total = nt_dot(stack, ones)
    carry = jnp.zeros((32, 128), F32)
    ridx = lax.broadcasted_iota(jnp.int32, (128, 128), 0).astype(F32)
    for t in range(8):
        rank = jnp.sum(parts[t] * (before[32 * t : 32 * t + 32] + carry), axis=0, keepdims=True)
        carry = carry + total[32 * t : 32 * t + 32]
        bt1[:, 128 * t : 128 * t + 128] = (ridx == rank).astype(BF16)
    a2 = jnp.concatenate([onehot * place_hi, onehot * place_lo], axis=0).astype(BF16)
    sent = nt_dot(a2, bt1[...])
    ssb[0] = sent[:32]
    ssb[1] = sent[32:]
    srb[:, 0:1, :] = ssb[:, pl.ds(gy, 1), :]


    c_v.wait()
    count = cnt[0]
    gram = jnp.zeros((96, 128), F32)
    for c in range(3):
        for q in range(6):
            lo = 512 * q
            keep = lax.broadcasted_iota(jnp.int32, (K, 512), 1) + lo < count
            x = jnp.where(keep, vv[c, :, lo : lo + 512], 0.0)
            hi, mid, low = split3(x)
            s = jnp.concatenate([hi, mid, low, jnp.zeros_like(hi)], axis=0).astype(BF16)
            gram = gram + nt_dot(s[:96], s)
    gram = gram[0:32] + gram[32:64] + gram[64:96]
    gram = gram + pltpu.roll(gram, 96, 1) + pltpu.roll(gram, 64, 1)
    lane32 = lax.broadcasted_iota(jnp.int32, (32, 128), 1)
    gram = jnp.where(lane32 < 32, gram, 0.0)
    packed = gram[0:8]
    for t in range(1, 4):
        packed = packed + pltpu.roll(gram[8 * t : 8 * t + 8], 32 * t, 1)
    gsb[...] = packed
    hrb[pl.ds(gx, 1)] = packed[None]
    to_line(gsb, hrb.at[gx], as_sem.at[3], ar_sem.at[3])

    pl.semaphore_wait(news.at[0], 4)
    for o in ((2, 0), (NZ - 2, 0)):
        pl.semaphore_signal(news.at[1], inc=1, device_id=(gx, peer(o)), device_id_type=MESH)

    for c in c_dg:
        c.wait()

    def recip(i, carry):
        for t in range(4):
            rv[t, i] = 1.0 / (6.0 + gd[t, i])
        return carry

    lax.fori_loop(0, 64, recip, 0, unroll=4)

    for (cond, dev, src, dst, there, here), mine in zip(faces, face_dst):
        @pl.when(cond)
        def _(dev=dev, src=src, mine=mine, here=here):
            remote(src, mine, fs_sem.at[here], fr_sem.at[here], dev).wait_recv()
    a_jm = jnp.where(jj == 0, pltpu.roll(fj[0], 1009, 1), 0.0)
    a_jp = jnp.where(jj == 15, pltpu.roll(fj[1], 15, 1), 0.0)
    lane1 = lax.broadcasted_iota(jnp.int32, (8, 128), 1)
    gap = jnp.zeros((8, 768), F32)
    a_i = jnp.concatenate(
        [
            jnp.where(lane1 < 16, pltpu.roll(fi[0], 16, 1), 0.0),
            gap,
            jnp.where(lane1 >= 112, pltpu.roll(fi[1], 112, 1), 0.0),
        ],
        axis=1,
    )
    corner = jnp.concatenate(
        [
            jnp.where(lane1 == 0, pltpu.roll(fc[0], 1, 1), 0.0)
            + jnp.where(lane1 == 15, pltpu.roll(fc[1], 31, 1), 0.0),
            gap,
            jnp.where(lane1 == 112, pltpu.roll(fc[2], 97, 1), 0.0)
            + jnp.where(lane1 == 127, pltpu.roll(fc[3], 127, 1), 0.0),
        ],
        axis=1,
    )
    P8 = num[0]
    D8 = num[1]
    R8 = num[2]
    once = (num[3] + a_jm + a_jp + a_i) * R8
    base = P8[7:8] + corner[7:8]
    beyond = (
        (a_jm[5:6] + base) * a_jm[4:5] + (a_jp[5:6] + base) * a_jp[4:5] + (a_i[5:6] + base) * a_i[4:5]
    )
    surface = (D8[7:8] + once[6:7] + lateral(once)[7:8] + beyond) * R8[7:8]
    c_n.wait()
    c_t.wait()
    forces = nrm[...] * surface + trc[...]

    pl.semaphore_wait(news.at[1], 2)
    to_group(lambda o: ssb.at[:, pl.ds(o, 1), :], lambda r: srb.at[:, r : r + 1, :], as_sem.at[0], lambda r: sl_sem.at[r // 8])

    onehot = ons[...]
    rows = []
    for piece in split3(forces):
        for c in range(3):
            rows.append((onehot * piece[c : c + 1]).astype(BF16))
    moved = nt_dot(jnp.concatenate(rows, axis=0), bt1[...])
    moved = moved[0:96] + moved[96:192] + moved[192:288]
    for c in range(3):
        fsb[c] = moved[32 * c : 32 * c + 32]
    frb[:, 0:1, :] = fsb[:, pl.ds(gy, 1), :]
    to_group(lambda o: fsb.at[:, pl.ds(o, 1), :], lambda r: frb.at[:, r : r + 1, :], as_sem.at[2], lambda r: gr_sem.at[r // 8])

    def slot_row(ref, c, h):
        return ref[16 * c + h // 2 : 16 * c + h // 2 + 1, 128 * (h % 2) : 128 * (h % 2) + 128]

    where = lax.broadcasted_iota(jnp.int32, (48, 256), 0)
    where = (where & 15) * 256 + lax.broadcasted_iota(jnp.int32, (48, 256), 1)
    occ[...] = (where < count).astype(F32)
    c_prev.wait()
    acc = [jnp.zeros((8, 128), F32) for _ in range(4)]
    for h in range(CAPR):
        lanes = slice(128 * h, 128 * h + 128)
        for c in range(3):
            res = slot_row(occ, c, h) * prv[c : c + 1, lanes]
            for k in range(4):
                acc[k] = acc[k] - vv[c, 8 * k : 8 * k + 8, lanes] * res
    for k in range(4):
        acc0[8 * k : 8 * k + 8] = acc[k]

    lane2 = lax.broadcasted_iota(jnp.int32, (16, 128), 1)

    def plane_sum(f, i):
        xs_ = [f[t, i + 1, 8:24, :] for t in range(4)]
        rr = [pltpu.roll(x, 1, 1) for x in xs_]
        rl = [pltpu.roll(x, 127, 1) for x in xs_]
        zero = jnp.zeros((16, 128), F32)
        res = []
        for t in range(4):
            down = jnp.where(lane2 == 0, rr[t - 1] if t > 0 else zero, rr[t])
            up = jnp.where(lane2 == 127, rl[t + 1] if t < 3 else zero, rl[t])
            s = f[t, i, 8:24, :] + f[t, i + 2, 8:24, :]
            s = s + (f[t, i + 1, 7:23, :] + f[t, i + 1, 9:25, :])
            res.append(dv[t, i] + s + (up + down))
        return res

    wait_halos(pp, 0)

    wait_bytes(hrb.at[pl.ds(0, ngx - 1)], ar_sem.at[3])
    packed = jnp.sum(hrb[...], axis=0)
    hsb[...] = packed
    gxb[pl.ds(gq, 1)] = packed[None]
    for d in (2, 1, 3):
        remote(hsb, gxb.at[gq], as_sem.at[1], ar_sem.at[1], (gx, gz * NX + wrap(gq + d, NX))).start()

    def sweep1(i, carry):
        sums = plane_sum(pp, i)
        for t in range(4):
            pq[t, i + 1, 8:24, :] = sums[t] * rv[t, i]
        return carry

    lax.fori_loop(0, 64, sweep1, 0, unroll=UNROLL)


    wait_bytes(gxb.at[pl.ds(0, 3)], ar_sem.at[1])
    packed = jnp.sum(gxb[...], axis=0)
    gxs[...] = packed
    grb[pl.ds(gz, 1)] = packed[None]
    for d in range(NZ - 1, 0, -1):
        e = (d + 1) // 2 if d % 2 else NZ - d // 2
        remote(gxs, grb.at[gz], as_sem.at[6], ar_sem.at[6], (gx, wrap(gz + e, NZ) * NX + gq)).start()

    hidx = lax.broadcasted_iota(jnp.int32, (16, 128), 0).astype(F32)
    lidx = lax.broadcasted_iota(jnp.int32, (256, 128), 0).astype(F32)

    def masks(g):
        first = max(8 * g, 1)
        wait_bytes(srb.at[:, first : 8 * g + 8, :], sl_sem.at[g])
        for b in range(8 * g, 8 * g + 8):
            lanes = slice(128 * b, 128 * b + 128)
            mh[:, lanes] = (hidx == srb[0, b : b + 1, :]).astype(F32)
            bt2[:, lanes] = (lidx == srb[1, b : b + 1, :]).astype(BF16)

    def place(g):
        first = max(8 * g, 1)
        wait_bytes(frb.at[:, first : 8 * g + 8, :], gr_sem.at[g])
        for c in range(3):
            pieces = split3(frb[c, 8 * g : 8 * g + 8, :])
            for b in range(8):
                lanes = slice(1024 * g + 128 * b, 1024 * g + 128 * b + 128)
                m = mh[:, lanes]
                for k in range(3):
                    r0 = 48 * k + 16 * c
                    amat[r0 : r0 + 16, lanes] = (m * pieces[k][b : b + 1]).astype(BF16)
        return nt_dot(amat[:, 1024 * g : 1024 * g + 1024], bt2[:, 1024 * g : 1024 * g + 1024])

    masks(0)
    masks(1)
    near[...] = place(0)
    masks(2)
    near[...] += place(1)
    masks(3)
    near[...] += place(2)

    own = near[...] + place(3)
    own = own[0:48] + own[48:96] + own[96:144]
    xs[...] = own
    msk[...] = own * occ[...]
    acc = [acc0[8 * k : 8 * k + 8] for k in range(4)]
    for h in range(CAPR):
        lanes = slice(128 * h, 128 * h + 128)
        for c in range(3):
            res = slot_row(msk, c, h)
            for k in range(4):
                acc[k] = acc[k] + vv[c, 8 * k : 8 * k + 8, lanes] * res
    diag = lax.broadcasted_iota(jnp.int32, (32, 128), 0) == lane32

    def to_row(col):
        return jnp.sum(jnp.where(diag, col, 0.0), axis=0, keepdims=True)

    def to_col(r):
        return jnp.sum(jnp.where(diag, r, 0.0), axis=1, keepdims=True)

    prow = to_row(jnp.sum(jnp.concatenate(acc, axis=0), axis=1, keepdims=True))
    psb[...] = prow
    prb[0:1, :] = prow
    to_group(lambda o: psb, lambda r: prb.at[r : r + 1, :], as_sem.at[4], lambda r: ar_sem.at[4])

    send_halos(pq, 4)

    wait_bytes(grb.at[pl.ds(0, NZ - 1)], ar_sem.at[6])
    packed = jnp.sum(grb[...], axis=0)
    m = jnp.concatenate([packed] + [pltpu.roll(packed, 128 - 32 * t, 1) for t in range(1, 4)], axis=0)
    sub32 = lax.broadcasted_iota(jnp.int32, (32, 128), 0)
    m = jnp.where(lane32 < 32, m, (sub32 + 32 == lane32).astype(F32))
    dinv = jnp.zeros((32, 1), F32)
    sub1 = lax.broadcasted_iota(jnp.int32, (32, 1), 0)
    for k in range(K):
        r = m[k : k + 1]
        inv = 1.0 / r[:, k : k + 1]
        dinv = jnp.where(sub1 == k, inv, dinv)
        if k < K - 1:
            f = jnp.where(sub1 > k, m[:, k : k + 1] * inv, 0.0)
            m = m - f * r
    linv = jnp.where(lane32 < 32, pltpu.roll(m, 96, 1), 0.0)

    wait_bytes(prb.at[1:ngy, :], ar_sem.at[4])
    prow = jnp.sum(prb[...], axis=0, keepdims=True)
    qsb[...] = prow
    qrb[pl.ds(gx, 1), :] = prow
    to_line(qsb, qrb.at[pl.ds(gx, 1), :], as_sem.at[5], ar_sem.at[5])
    wait_halos(pq, 4)

    def sweep2(i, carry):
        sums = plane_sum(pq, i)
        for t in range(4):
            out_p[i, :, 128 * t : 128 * t + 128] = sums[t] * rv[t, i]
        return carry

    lax.fori_loop(0, 64, sweep2, 0, unroll=UNROLL)

    c_w.wait()
    wait_bytes(qrb.at[pl.ds(0, ngx - 1), :], ar_sem.at[5])
    prow = jnp.sum(qrb[...], axis=0, keepdims=True)
    y = jnp.sum(linv * prow, axis=1, keepdims=True) * dinv
    cof[...] = jnp.broadcast_to(to_col(-jnp.sum(linv * y, axis=0, keepdims=True)), (32, 128))

    for cond, dev, src, dst, there, here in faces:
        @pl.when(cond)
        def _(dev=dev, src=src, dst=dst, here=here):
            remote(src, dst, fs_sem.at[here], fr_sem.at[here], dev).wait_send()
    wait_halos_sent(pp, 0)
    wait_halos_sent(pq, 4)
    wait_bytes(srb.at[:, 1:ngy, :], as_sem.at[0])
    wait_bytes(gxb.at[pl.ds(0, 3)], as_sem.at[1])
    wait_bytes(grb.at[pl.ds(0, NZ - 1)], as_sem.at[6])
    wait_bytes(frb.at[:, 1:ngy, :], as_sem.at[2])
    wait_bytes(hrb.at[pl.ds(0, ngx - 1)], as_sem.at[3])
    wait_bytes(prb.at[1:ngy, :], as_sem.at[4])
    wait_bytes(qrb.at[pl.ds(0, ngx - 1), :], as_sem.at[5])


def finish(p_new, ww, xs, occ, cof, out_p, out_c, outc, sem):
    c_p = pltpu.make_async_copy(p_new, out_p, sem.at[0])
    c_p.start()
    cb = [cof[8 * k : 8 * k + 8, :] for k in range(4)]
    for h in range(24):
        lanes = slice(128 * h, 128 * h + 128)
        half = slice(128 * (h % 2), 128 * (h % 2) + 128)
        for c in range(3):
            u = cb[0] * ww[c, 0:8, lanes] + cb[1] * ww[c, 8:16, lanes]
            u = u + (cb[2] * ww[c, 16:24, lanes] + cb[3] * ww[c, 24:32, lanes])
            u = jnp.sum(u, axis=0, keepdims=True)
            r = 16 * c + h // 2
            outc[c : c + 1, lanes] = occ[r : r + 1, half] * (xs[r : r + 1, half] + u)
    c_c = pltpu.make_async_copy(outc, out_c, sem.at[1])
    c_c.start()
    c_p.wait()
    c_c.wait()


def shards(
    ngx, ngy,
    pressure, divergence, diagonal, normals, traction, slot_of, counts, previous, secant_v, secant_w,
):
    v = jnp.transpose(secant_v, (1, 0, 2))
    w = jnp.transpose(secant_w, (1, 0, 2))
    def in_hbm(x):
        return pltpu.with_memory_space_constraint(x, pltpu.HBM)

    hbm = pl.BlockSpec(memory_space=pltpu.HBM)
    vmem = pl.BlockSpec(memory_space=pltpu.VMEM)
    vm = pltpu.VMEM
    dma = pltpu.SemaphoreType.DMA
    p_new, w_in, own, occ, coef = pl.pallas_call(
        functools.partial(kernel, ngx, ngy),
        out_shape=(
            jax.ShapeDtypeStruct(pressure.shape, F32),
            jax.ShapeDtypeStruct(w.shape, F32),
            jax.ShapeDtypeStruct((48, 256), F32),
            jax.ShapeDtypeStruct((48, 256), F32),
            jax.ShapeDtypeStruct((32, 128), F32),
        ),
        in_specs=[hbm] * 6 + [pl.BlockSpec(memory_space=pltpu.SMEM)] + [hbm] * 3,
        out_specs=(vmem,) * 5,
        scratch_shapes=[
            vm((4, 66, 32, 128), F32),
            vm((4, 66, 32, 128), F32),
            vm((4, 64, 16, 128), F32),
            vm((4, 64, 16, 128), F32),
            vm((4, 64, 16, 128), F32),
                vm((3, 32, 3072), F32),
            vm((3, 1024), F32),
            vm((3, 1024), F32),
            vm((1, 1024), jnp.int32),
                vm((3, 3072), F32),
                vm((8, 1024), F32),
            vm((4, 8, 1024), F32),
            vm((32, 1024), F32),
            vm((128, 1024), BF16),
            vm((16, 128 * ngy), F32),
            vm((256, 128 * ngy), BF16),
            vm((144, 128 * ngy), BF16),
            vm((2, 8, 1024), F32),
            vm((2, 8, 128), F32),
            vm((4, 8, 128), F32),
            vm((2, 32, 128), F32),
            vm((2, 32, 128), F32),
            vm((3, 32, 128), F32),
            vm((3, 32, 128), F32),
            vm((144, 256), F32),
            vm((48, 256), F32),
            vm((32, 128), F32),
            vm((8, 128), F32),
            vm((4, 8, 128), F32),
            vm((8, 128), F32),
            vm((ngy // 4, 8, 128), F32),
            vm((8, 128), F32),
            vm((ngx, 8, 128), F32),
            vm((1, 128), F32),
            vm((ngy, 128), F32),
            vm((1, 128), F32),
            vm((ngx, 128), F32),
            dma((24,)),
            dma((8,)),
            dma((8,)),
            dma((8,)),
            dma((8,)),
            dma((7,)),
            dma((7,)),
            dma((4,)),
            dma((4,)),
            pltpu.SemaphoreType.REGULAR((2,)),
        ],
        compiler_params=pltpu.CompilerParams(
            collective_id=0, has_side_effects=True, vmem_limit_bytes=48 * 1024 * 1024
        ),
    )(
        in_hbm(pressure), in_hbm(divergence), in_hbm(diagonal), in_hbm(normals), in_hbm(traction), in_hbm(slot_of),
        counts, in_hbm(previous), in_hbm(v), in_hbm(w),
    )
    return pl.pallas_call(
        finish,
        out_shape=(
            jax.ShapeDtypeStruct(pressure.shape, F32),
            jax.ShapeDtypeStruct(previous.shape, F32),
        ),
        in_specs=[vmem] * 5,
        out_specs=(hbm, hbm),
        scratch_shapes=[vm((3, 3072), F32), dma((2,))],
        compiler_params=pltpu.CompilerParams(vmem_limit_bytes=4 * 1024 * 1024),
    )(p_new, w_in, own, occ, coef)


def solution(mesh):
    placed = (
        P("gx", "gy", None),
        P("gx", "gy", None),
        P("gx", "gy", None),
        P(None, ("gx", "gy")),
        P(None, ("gx", "gy")),
        P("gx", None),
        P(("gx", "gy")),
        P(None, ("gx", "gy")),
        P(None, None, ("gx", "gy")),
        P(None, None, ("gx", "gy")),
    )
    return jax.shard_map(
        functools.partial(shards, mesh.shape["gx"], mesh.shape["gy"]),
        mesh=mesh,
        in_specs=placed,
        out_specs=(P("gx", "gy", None), P(None, ("gx", "gy"))),
        check_vma=False,
    )
```

time: 47.2 us -> 35.3 us (0.75)
  the two profiles are of different devices: /device:TPU:32 before, /device:TPU:1 now
where the time goes in v2:
time: 35.3 us; the launch traced here: 35.2 us
  Pallas kernels  33.9 us (96%)
  between operations  1.29 us (4%)
    pallas_call x1, Pallas kernels, shards(): pl.pallas_call(functools.partial(kernel, ngx, ngy), out_shape=(jax.ShapeD...  32.6 us
    pallas_call x1, Pallas kernels, shards(): pl.pallas_call(finish, out_shape=(jax.ShapeDtypeStruct(pressure.shape, F3...  1.34 us

profile of v2, /device:TPU:1, one launch (start us, length us, event | category | flops | bytes accessed | tf_op | source)
XLA Modules:
  0.0 35.2 jit_solution(2214752139079267202)
XLA Ops:
  1.3 32.6 %shard_map.113 = (f32[64,16,512]{2,1,0:T(8,128)S(1)}, f32[3,32,3072]{2,1,0:T(8,128)S(1)}, f32[48,256]{1,0:T(8,128)S(1)}, f32[48,256]{1,0:T(8,128)S(1)}, f32[32,128]{1,0:T(8,128)S(1)}) custom-call(f32[64,16,512]{2,1,0:T(8,128)} %p_hbm.1, f32[64,16,512]{2,1,0:T(8,128)} %d_hbm.1, f32[64,16,512]{2,1,0:T(8,128)} %g_hbm.1, f32[3,1024]{1,0:T(4,128)} %n_hbm.1, ...), custom_call_target="tpu_custom_call" | custom-call | tf_op jit(solution)/shard_map/pallas_call | solution.py:533
  33.9 1.3 %shard_map.114 = (f32[64,16,512]{2,1,0:T(8,128)}, f32[3,3072]{1,0:T(4,128)}) custom-call(f32[64,16,512]{2,1,0:T(8,128)S(1)} %get-tuple-element.7.p_new, f32[3,32,3072]{2,1,0:T(8,128)S(1)} %get-tuple-element.8.ww, f32[48,256]{1,0:T(8,128)S(1)} %get-tuple-element.9.xs, f32[48,256]{1,0:T(8,128)S(1)} %get-tuple-element.10.occ, f32[32,128]{1,0:T(8,128)S(1)} %get-tuple-element.11.cof), custom_call_target="tpu_custom_call" | custom-call | tf_op jit(solution)/shard_map/pallas_call | solution.py:600

commit v3 on v2

--- a/solution.py
+++ b/solution.py
@@ -24,19 +24,25 @@
     return hi, mid, rest - mid
 
 
+def split2(x):
+    hi = x.astype(BF16).astype(F32)
+    return hi, x - hi
+
+
 def kernel(
     ngx, ngy,
-    p_hbm, d_hbm, g_hbm, n_hbm, t_hbm, slot_hbm, cnt, prev_hbm, v_hbm, w_hbm,
+    p_hbm, d_hbm, g_hbm, n_hbm, t_hbm, slot_hbm, grp_hbm, prev_hbm, v_hbm, w_hbm,
     out_p, ww, xs, occ, cof,
-    pp, pq, dv, gd, rv, vv, nrm, trc, slt, prv,
+    pp, pq, dv, gd, rv, vv, nrm, trc, slt, grp, prv,
     slab, num, ons, bt1, mh, bt2, amat,
-    fj, fi, fc, ssb, srb, fsb, frb, near, msk, acc0, gsb, gxb, gxs, grb, hsb, hrb, psb, prb, qsb, qrb,
+    fj, fi, fc, ssb, srb, plc, fsb, frb, near, msk, acc0, gsb, gxb, gxs, grb, hsb, hrb, psb, prb, qsb, qrb,
     in_sem, fs_sem, fr_sem, hs_sem, hr_sem, as_sem, ar_sem, gr_sem, sl_sem, news,
 ):
     gx = lax.axis_index("gx")
     gy = lax.axis_index("gy")
     K = 32
     UNROLL = 4
+    NEAR = 24
     CAPR = 24
 
     NZ, NX = ngy // 4, 4
@@ -72,11 +78,10 @@
         load(g_hbm.at[:, :, lanes_of(3)], gd.at[3]),
     )
     bar = pltpu.get_barrier_semaphore()
-    greet = [
-        (wrap(gx + a, ngx), wrap(gy + b, ngy)) for a in (-1, 0, 1) for b in (-1, 0, 1) if (a, b) != (0, 0)
-    ]
-    greet += [(gx, peer(o)) for o in ((1, 0), (NZ - 1, 0), (2, 0), (NZ - 2, 0), (0, 1), (0, 3), (0, 2))]
-    greet += [(wrap(gx + a, ngx), gy) for a in range(2, ngx - 1)]
+    greet = [(wrap(gx + a, ngx), wrap(gy + b, ngy)) for a in (-1, 1) for b in (-1, 1)]
+    greet += [(gx, peer(o)) for o in ((2, 0), (NZ - 2, 0), (0, 2), (1, 0), (NZ - 1, 0), (0, 1), (0, 3))]
+    greet += [(gx, wrap(gy + b, ngy)) for b in (-1, 1)]
+    greet += [(wrap(gx + a, ngx), gy) for a in range(1, ngx)]
     for dev in greet:
         pl.semaphore_signal(bar, inc=1, device_id=dev, device_id_type=MESH)
 
@@ -84,6 +89,7 @@
     c_p = [load_p(t) for t in range(3)]
     c_n = load(n_hbm, nrm)
     c_t = load(t_hbm, trc)
+    c_grp = load(grp_hbm, grp)
     c_v = load(v_hbm, vv)
     c_dg = [load(d_hbm.at[:, :, lanes_of(t)], dv.at[t]) for t in range(3)]
     c_dg += [load(g_hbm.at[:, :, lanes_of(t)], gd.at[t]) for t in range(3)]
@@ -101,11 +107,6 @@
         def _():
             ref[...] = jnp.zeros(ref.shape, ref.dtype)
 
-    for f in (pp, pq):
-        zero_when(has_im, f.at[:, 0:1, 8:24, :])
-        zero_when(has_ip, f.at[:, 65:66, 8:24, :])
-        zero_when(has_jm, f.at[:, 1:65, 7:8, :])
-        zero_when(has_jp, f.at[:, 1:65, 24:25, :])
     zero_when(has_jm, fj.at[0])
     zero_when(has_jp, fj.at[1])
     zero_when(has_im, fi.at[0])
@@ -197,17 +198,13 @@
 
     pl.semaphore_wait(bar, len(greet))
 
-    for cond, dev, src, dst, there, here in faces:
+    for cond, dev, src, dst, there, here in faces[4:] + faces[:4]:
         @pl.when(cond)
         def _(dev=dev, src=src, dst=dst, there=there, here=here):
             remote(src, dst, fs_sem.at[here], fr_sem.at[there], dev).start()
 
     for o in ((1, 0), (NZ - 1, 0), (2, 0), (NZ - 2, 0)):
         pl.semaphore_signal(news.at[0], inc=1, device_id=(gx, peer(o)), device_id_type=MESH)
-
-    for c in c_p:
-        c.wait()
-    send_halos(pp, 0)
 
     c_slot.wait()
     slot = slt[...].astype(F32)
@@ -234,18 +231,31 @@
         bt1[:, 128 * t : 128 * t + 128] = (ridx == rank).astype(BF16)
     a2 = jnp.concatenate([onehot * place_hi, onehot * place_lo], axis=0).astype(BF16)
     sent = nt_dot(a2, bt1[...])
-    ssb[0] = sent[:32]
-    ssb[1] = sent[32:]
-    srb[:, 0:1, :] = ssb[:, pl.ds(gy, 1), :]
-
-
+    ssb[...] = sent[:32] * 256.0 + sent[32:]
+    srb[0:1, :] = ssb[pl.ds(gy, 1), :]
+    fsb[pl.ds(3, 32, stride=4), :] = jnp.zeros((32, 128), F32)
+
+
+    for c in c_p:
+        c.wait()
+    send_halos(pp, 0)
+
+    for f in (pp, pq):
+        zero_when(has_im, f.at[:, 0:1, 8:24, :])
+        zero_when(has_ip, f.at[:, 65:66, 8:24, :])
+        zero_when(has_jm, f.at[:, 1:65, 7:8, :])
+        zero_when(has_jp, f.at[:, 1:65, 24:25, :])
     c_v.wait()
-    count = cnt[0]
+    c_grp.wait()
+    first_place = gy * 3072
+    mine = jnp.logical_and(grp[...] >= first_place, grp[...] < first_place + 3072).astype(F32)
+    mine = mine.reshape(ngy, 8, 128)
+    count = jnp.sum(jnp.sum(jnp.sum(mine, axis=0), axis=0, keepdims=True), axis=1, keepdims=True)
     gram = jnp.zeros((96, 128), F32)
     for c in range(3):
         for q in range(6):
             lo = 512 * q
-            keep = lax.broadcasted_iota(jnp.int32, (K, 512), 1) + lo < count
+            keep = (lax.broadcasted_iota(jnp.int32, (K, 512), 1) + lo).astype(F32) < count
             x = jnp.where(keep, vv[c, :, lo : lo + 512], 0.0)
             hi, mid, low = split3(x)
             s = jnp.concatenate([hi, mid, low, jnp.zeros_like(hi)], axis=0).astype(BF16)
@@ -274,6 +284,9 @@
         return carry
 
     lax.fori_loop(0, 64, recip, 0, unroll=4)
+
+    pl.semaphore_wait(news.at[1], 2)
+    to_group(lambda o: ssb.at[pl.ds(o, 1), :], lambda r: srb.at[r : r + 1, :], as_sem.at[0], lambda r: sl_sem.at[int(r >= NEAR)])
 
     for (cond, dev, src, dst, there, here), mine in zip(faces, face_dst):
         @pl.when(cond)
@@ -314,27 +327,24 @@
     c_t.wait()
     forces = nrm[...] * surface + trc[...]
 
-    pl.semaphore_wait(news.at[1], 2)
-    to_group(lambda o: ssb.at[:, pl.ds(o, 1), :], lambda r: srb.at[:, r : r + 1, :], as_sem.at[0], lambda r: sl_sem.at[r // 8])
-
     onehot = ons[...]
     rows = []
-    for piece in split3(forces):
+    for piece in split2(forces):
         for c in range(3):
             rows.append((onehot * piece[c : c + 1]).astype(BF16))
     moved = nt_dot(jnp.concatenate(rows, axis=0), bt1[...])
-    moved = moved[0:96] + moved[96:192] + moved[192:288]
+    moved = moved[0:96] + moved[96:192]
     for c in range(3):
-        fsb[c] = moved[32 * c : 32 * c + 32]
-    frb[:, 0:1, :] = fsb[:, pl.ds(gy, 1), :]
-    to_group(lambda o: fsb.at[:, pl.ds(o, 1), :], lambda r: frb.at[:, r : r + 1, :], as_sem.at[2], lambda r: gr_sem.at[r // 8])
+        fsb[pl.ds(c, 32, stride=4), :] = moved[32 * c : 32 * c + 32]
+    frb[0:4, :] = fsb[pl.ds(pl.multiple_of(4 * gy, 4), 4), :]
+    to_group(lambda o: fsb.at[pl.ds(pl.multiple_of(4 * o, 4), 4), :], lambda r: frb.at[4 * r : 4 * r + 4, :], as_sem.at[2], lambda r: gr_sem.at[int(r >= NEAR)])
 
     def slot_row(ref, c, h):
         return ref[16 * c + h // 2 : 16 * c + h // 2 + 1, 128 * (h % 2) : 128 * (h % 2) + 128]
 
     where = lax.broadcasted_iota(jnp.int32, (48, 256), 0)
     where = (where & 15) * 256 + lax.broadcasted_iota(jnp.int32, (48, 256), 1)
-    occ[...] = (where < count).astype(F32)
+    occ[...] = (where.astype(F32) < count).astype(F32)
     c_prev.wait()
     acc = [jnp.zeros((8, 128), F32) for _ in range(4)]
     for h in range(CAPR):
@@ -345,6 +355,13 @@
                 acc[k] = acc[k] - vv[c, 8 * k : 8 * k + 8, lanes] * res
     for k in range(4):
         acc0[8 * k : 8 * k + 8] = acc[k]
+
+    wait_bytes(hrb.at[pl.ds(0, ngx - 1)], ar_sem.at[3])
+    packed = jnp.sum(hrb[...], axis=0)
+    hsb[...] = packed
+    gxb[pl.ds(gq, 1)] = packed[None]
+    for d in (2, 1, 3):
+        remote(hsb, gxb.at[gq], as_sem.at[1], ar_sem.at[1], (gx, gz * NX + wrap(gq + d, NX))).start()
 
     lane2 = lax.broadcasted_iota(jnp.int32, (16, 128), 1)
 
@@ -364,13 +381,6 @@
 
     wait_halos(pp, 0)
 
-    wait_bytes(hrb.at[pl.ds(0, ngx - 1)], ar_sem.at[3])
-    packed = jnp.sum(hrb[...], axis=0)
-    hsb[...] = packed
-    gxb[pl.ds(gq, 1)] = packed[None]
-    for d in (2, 1, 3):
-        remote(hsb, gxb.at[gq], as_sem.at[1], ar_sem.at[1], (gx, gz * NX + wrap(gq + d, NX))).start()
-
     def sweep1(i, carry):
         sums = plane_sum(pp, i)
         for t in range(4):
@@ -389,39 +399,42 @@
         remote(gxs, grb.at[gz], as_sem.at[6], ar_sem.at[6], (gx, wrap(gz + e, NZ) * NX + gq)).start()
 
     hidx = lax.broadcasted_iota(jnp.int32, (16, 128), 0).astype(F32)
-    lidx = lax.broadcasted_iota(jnp.int32, (256, 128), 0).astype(F32)
-
-    def masks(g):
-        first = max(8 * g, 1)
-        wait_bytes(srb.at[:, first : 8 * g + 8, :], sl_sem.at[g])
-        for b in range(8 * g, 8 * g + 8):
+    lidx = [(lax.broadcasted_iota(jnp.int32, (16, 128), 0) + 16 * k).astype(F32).astype(BF16) for k in range(16)]
+    one, zero = jnp.ones((16, 128), BF16), jnp.zeros((16, 128), BF16)
+
+    def masks(g, lo, hi):
+        wait_bytes(srb.at[max(lo, 1) : hi, :], sl_sem.at[g])
+        place = srb[lo:hi, :]
+        place_hi = jnp.floor((place + 0.5) * (1.0 / 256.0))
+        plc[0, lo:hi, :] = place_hi
+        plc[1, lo:hi, :] = place - place_hi * 256.0
+        for b in range(lo, hi):
             lanes = slice(128 * b, 128 * b + 128)
-            mh[:, lanes] = (hidx == srb[0, b : b + 1, :]).astype(F32)
-            bt2[:, lanes] = (lidx == srb[1, b : b + 1, :]).astype(BF16)
-
-    def place(g):
-        first = max(8 * g, 1)
-        wait_bytes(frb.at[:, first : 8 * g + 8, :], gr_sem.at[g])
+            mh[:, lanes] = (hidx == plc[0, b : b + 1, :]).astype(F32)
+            low = jnp.broadcast_to(plc[1, b : b + 1, :], (16, 128)).astype(BF16)
+            for k in range(16):
+                bt2[16 * k : 16 * k + 16, lanes] = jnp.where(lidx[k] == low, one, zero)
+
+    def place(g, lo, hi):
+        wait_bytes(frb.at[4 * max(lo, 1) : 4 * hi, :], gr_sem.at[g])
         for c in range(3):
-            pieces = split3(frb[c, 8 * g : 8 * g + 8, :])
-            for b in range(8):
-                lanes = slice(1024 * g + 128 * b, 1024 * g + 128 * b + 128)
-                m = mh[:, lanes]
-                for k in range(3):
-                    r0 = 48 * k + 16 * c
-                    amat[r0 : r0 + 16, lanes] = (m * pieces[k][b : b + 1]).astype(BF16)
-        return nt_dot(amat[:, 1024 * g : 1024 * g + 1024], bt2[:, 1024 * g : 1024 * g + 1024])
-
-    masks(0)
-    masks(1)
-    near[...] = place(0)
-    masks(2)
-    near[...] += place(1)
-    masks(3)
-    near[...] += place(2)
-
-    own = near[...] + place(3)
-    own = own[0:48] + own[48:96] + own[96:144]
+            for b0 in range(lo, hi, 8):
+                pieces = split2(frb[pl.ds(4 * b0 + c, 8, stride=4), :])
+                for b in range(8):
+                    lanes = slice(128 * (b0 + b), 128 * (b0 + b) + 128)
+                    m = mh[:, lanes]
+                    for k in range(2):
+                        r0 = 48 * k + 16 * c
+                        amat[r0 : r0 + 16, lanes] = (m * pieces[k][b : b + 1]).astype(BF16)
+        lanes = slice(128 * lo, 128 * hi)
+        return nt_dot(amat[:, lanes], bt2[:, lanes])
+
+    masks(0, 0, NEAR)
+    masks(1, NEAR, ngy)
+    near[...] = place(0, 0, NEAR)
+
+    own = near[...] + place(1, NEAR, ngy)
+    own = own[0:48] + own[48:96]
     xs[...] = own
     msk[...] = own * occ[...]
     acc = [acc0[8 * k : 8 * k + 8] for k in range(4)]
@@ -489,10 +502,10 @@
             remote(src, dst, fs_sem.at[here], fr_sem.at[here], dev).wait_send()
     wait_halos_sent(pp, 0)
     wait_halos_sent(pq, 4)
-    wait_bytes(srb.at[:, 1:ngy, :], as_sem.at[0])
+    wait_bytes(srb.at[1:ngy, :], as_sem.at[0])
     wait_bytes(gxb.at[pl.ds(0, 3)], as_sem.at[1])
     wait_bytes(grb.at[pl.ds(0, NZ - 1)], as_sem.at[6])
-    wait_bytes(frb.at[:, 1:ngy, :], as_sem.at[2])
+    wait_bytes(frb.at[4 : 4 * ngy, :], as_sem.at[2])
     wait_bytes(hrb.at[pl.ds(0, ngx - 1)], as_sem.at[3])
     wait_bytes(prb.at[1:ngy, :], as_sem.at[4])
     wait_bytes(qrb.at[pl.ds(0, ngx - 1), :], as_sem.at[5])
@@ -539,7 +552,7 @@
             jax.ShapeDtypeStruct((48, 256), F32),
             jax.ShapeDtypeStruct((32, 128), F32),
         ),
-        in_specs=[hbm] * 6 + [pl.BlockSpec(memory_space=pltpu.SMEM)] + [hbm] * 3,
+        in_specs=[hbm] * 10,
         out_specs=(vmem,) * 5,
         scratch_shapes=[
             vm((4, 66, 32, 128), F32),
@@ -551,6 +564,7 @@
             vm((3, 1024), F32),
             vm((3, 1024), F32),
             vm((1, 1024), jnp.int32),
+            vm((8 * ngy, 128), jnp.int32),
                 vm((3, 3072), F32),
                 vm((8, 1024), F32),
             vm((4, 8, 1024), F32),
@@ -558,15 +572,16 @@
             vm((128, 1024), BF16),
             vm((16, 128 * ngy), F32),
             vm((256, 128 * ngy), BF16),
-            vm((144, 128 * ngy), BF16),
+            vm((96, 128 * ngy), BF16),
             vm((2, 8, 1024), F32),
             vm((2, 8, 128), F32),
             vm((4, 8, 128), F32),
-            vm((2, 32, 128), F32),
-            vm((2, 32, 128), F32),
-            vm((3, 32, 128), F32),
-            vm((3, 32, 128), F32),
-            vm((144, 256), F32),
+            vm((32, 128), F32),
+            vm((ngy, 128), F32),
+            vm((2, ngy, 128), F32),
+            vm((128, 128), F32),
+            vm((128, 128), F32),
+            vm((96, 256), F32),
             vm((48, 256), F32),
             vm((32, 128), F32),
             vm((8, 128), F32),
@@ -586,8 +601,8 @@
             dma((8,)),
             dma((7,)),
             dma((7,)),
-            dma((4,)),
-            dma((4,)),
+            dma((2,)),
+            dma((2,)),
             pltpu.SemaphoreType.REGULAR((2,)),
         ],
         compiler_params=pltpu.CompilerParams(
@@ -595,7 +610,7 @@
         ),
     )(
         in_hbm(pressure), in_hbm(divergence), in_hbm(diagonal), in_hbm(normals), in_hbm(traction), in_hbm(slot_of),
-        counts, in_hbm(previous), in_hbm(v), in_hbm(w),
+        in_hbm(slot_of.reshape(8 * ngy, 128)), in_hbm(previous), in_hbm(v), in_hbm(w),
     )
     return pl.pallas_call(
         finish,

time: 35.3 us -> 34 us (0.963)
  Pallas kernels: 33.9 us -> 33.2 us
  between operations: 1.29 us -> 0.64 us
    pallas_call x1, Pallas kernels: 32.6 us -> 31.9 us  [shards(): pl.pallas_call(functools.partial(kernel, ngx, ngy), out_shape=(jax.ShapeD...]
where the time goes in v3:
time: 34 us; the launch traced here: 33.9 us
  Pallas kernels  33.2 us (98%)
  between operations  0.64 us (2%)
    pallas_call x1, Pallas kernels, shards(): pl.pallas_call(functools.partial(kernel, ngx, ngy), out_shape=(jax.ShapeD...  31.9 us
    pallas_call x1, Pallas kernels, shards(): pl.pallas_call(finish, out_shape=(jax.ShapeDtypeStruct(pressure.shape, F3...  1.34 us

profile of v3, /device:TPU:1, one launch (start us, length us, event | category | flops | bytes accessed | tf_op | source)
XLA Modules:
  0.0 33.9 jit_solution(4000768100909209431)
XLA Ops:
  0.6 31.9 %shard_map.104 = (f32[64,16,512]{2,1,0:T(8,128)S(1)}, f32[3,32,3072]{2,1,0:T(8,128)S(1)}, f32[48,256]{1,0:T(8,128)S(1)}, f32[48,256]{1,0:T(8,128)S(1)}, f32[32,128]{1,0:T(8,128)S(1)}) custom-call(f32[64,16,512]{2,1,0:T(8,128)} %p_hbm.1, f32[64,16,512]{2,1,0:T(8,128)} %d_hbm.1, f32[64,16,512]{2,1,0:T(8,128)} %g_hbm.1, f32[3,1024]{1,0:T(4,128)} %n_hbm.1, ...), custom_call_target="tpu_custom_call" | custom-call | tf_op jit(solution)/shard_map/pallas_call | solution.py:546
  32.5 1.3 %shard_map.105 = (f32[64,16,512]{2,1,0:T(8,128)}, f32[3,3072]{1,0:T(4,128)}) custom-call(f32[64,16,512]{2,1,0:T(8,128)S(1)} %get-tuple-element.7.p_new, f32[3,32,3072]{2,1,0:T(8,128)S(1)} %get-tuple-element.8.ww, f32[48,256]{1,0:T(8,128)S(1)} %get-tuple-element.9.xs, f32[48,256]{1,0:T(8,128)S(1)} %get-tuple-element.10.occ, f32[32,128]{1,0:T(8,128)S(1)} %get-tuple-element.11.cof), custom_call_target="tpu_custom_call" | custom-call | tf_op jit(solution)/shard_map/pallas_call | solution.py:615

commit v4 on v3

--- a/solution.py
+++ b/solution.py
@@ -32,7 +32,7 @@
 def kernel(
     ngx, ngy,
     p_hbm, d_hbm, g_hbm, n_hbm, t_hbm, slot_hbm, grp_hbm, prev_hbm, v_hbm, w_hbm,
-    out_p, ww, xs, occ, cof,
+    out_p, ww, xs, occ, lnv, dnv, prj,
     pp, pq, dv, gd, rv, vv, nrm, trc, slt, grp, prv,
     slab, num, ons, bt1, mh, bt2, amat,
     fj, fi, fc, ssb, srb, plc, fsb, frb, near, msk, acc0, gsb, gxb, gxs, grb, hsb, hrb, psb, prb, qsb, qrb,
@@ -140,7 +140,7 @@
             remote(src_of(o), dst_of(r), ss, rs_of(r), (gx, o)).start()
 
     def to_line(src, dst, ss, rs):
-        for d in range(1, ngx):
+        for d in sorted(range(1, ngx), key=lambda d: abs(2 * d - ngx)):
             remote(src, dst, ss, rs, (wrap(gx + d, ngx), gy)).start()
 
     def wait_bytes(ref, sem):
@@ -449,9 +449,6 @@
     def to_row(col):
         return jnp.sum(jnp.where(diag, col, 0.0), axis=0, keepdims=True)
 
-    def to_col(r):
-        return jnp.sum(jnp.where(diag, r, 0.0), axis=1, keepdims=True)
-
     prow = to_row(jnp.sum(jnp.concatenate(acc, axis=0), axis=1, keepdims=True))
     psb[...] = prow
     prb[0:1, :] = prow
@@ -473,7 +470,8 @@
         if k < K - 1:
             f = jnp.where(sub1 > k, m[:, k : k + 1] * inv, 0.0)
             m = m - f * r
-    linv = jnp.where(lane32 < 32, pltpu.roll(m, 96, 1), 0.0)
+    lnv[...] = jnp.where(lane32 < 32, pltpu.roll(m, 96, 1), 0.0)
+    dnv[...] = jnp.broadcast_to(dinv, (32, 128))
 
     wait_bytes(prb.at[1:ngy, :], ar_sem.at[4])
     prow = jnp.sum(prb[...], axis=0, keepdims=True)
@@ -492,9 +490,7 @@
 
     c_w.wait()
     wait_bytes(qrb.at[pl.ds(0, ngx - 1), :], ar_sem.at[5])
-    prow = jnp.sum(qrb[...], axis=0, keepdims=True)
-    y = jnp.sum(linv * prow, axis=1, keepdims=True) * dinv
-    cof[...] = jnp.broadcast_to(to_col(-jnp.sum(linv * y, axis=0, keepdims=True)), (32, 128))
+    prj[...] = qrb[...]
 
     for cond, dev, src, dst, there, here in faces:
         @pl.when(cond)
@@ -511,10 +507,16 @@
     wait_bytes(qrb.at[pl.ds(0, ngx - 1), :], as_sem.at[5])
 
 
-def finish(p_new, ww, xs, occ, cof, out_p, out_c, outc, sem):
+def finish(p_new, ww, xs, occ, lnv, dnv, prj, out_p, out_c, outc, sem):
     c_p = pltpu.make_async_copy(p_new, out_p, sem.at[0])
     c_p.start()
-    cb = [cof[8 * k : 8 * k + 8, :] for k in range(4)]
+    linv = lnv[...]
+    prow = jnp.sum(prj[...], axis=0, keepdims=True)
+    y = jnp.sum(linv * prow, axis=1, keepdims=True) * dnv[...]
+    crow = -jnp.sum(linv * y, axis=0, keepdims=True)
+    diag = lax.broadcasted_iota(jnp.int32, (32, 128), 0) == lax.broadcasted_iota(jnp.int32, (32, 128), 1)
+    coef = jnp.broadcast_to(jnp.sum(jnp.where(diag, crow, 0.0), axis=1, keepdims=True), (32, 128))
+    cb = [coef[8 * k : 8 * k + 8, :] for k in range(4)]
     for h in range(24):
         lanes = slice(128 * h, 128 * h + 128)
         half = slice(128 * (h % 2), 128 * (h % 2) + 128)
@@ -543,7 +545,7 @@
     vmem = pl.BlockSpec(memory_space=pltpu.VMEM)
     vm = pltpu.VMEM
     dma = pltpu.SemaphoreType.DMA
-    p_new, w_in, own, occ, coef = pl.pallas_call(
+    p_new, *rest = pl.pallas_call(
         functools.partial(kernel, ngx, ngy),
         out_shape=(
             jax.ShapeDtypeStruct(pressure.shape, F32),
@@ -551,9 +553,11 @@
             jax.ShapeDtypeStruct((48, 256), F32),
             jax.ShapeDtypeStruct((48, 256), F32),
             jax.ShapeDtypeStruct((32, 128), F32),
+            jax.ShapeDtypeStruct((32, 128), F32),
+            jax.ShapeDtypeStruct((ngx, 128), F32),
         ),
         in_specs=[hbm] * 10,
-        out_specs=(vmem,) * 5,
+        out_specs=(vmem,) * 7,
         scratch_shapes=[
             vm((4, 66, 32, 128), F32),
             vm((4, 66, 32, 128), F32),
@@ -618,11 +622,11 @@
             jax.ShapeDtypeStruct(pressure.shape, F32),
             jax.ShapeDtypeStruct(previous.shape, F32),
         ),
-        in_specs=[vmem] * 5,
+        in_specs=[vmem] * 7,
         out_specs=(hbm, hbm),
         scratch_shapes=[vm((3, 3072), F32), dma((2,))],
         compiler_params=pltpu.CompilerParams(vmem_limit_bytes=4 * 1024 * 1024),
-    )(p_new, w_in, own, occ, coef)
+    )(p_new, *rest)
 
 
 def solution(mesh):

time: 34 us -> 33.7 us (level)
  no operation moved by 1% of the time
where the time goes in v4:
time: 33.7 us; the launch traced here: 33.6 us
  Pallas kernels  33 us (98%)
  between operations  0.64 us (2%)
    pallas_call x1, Pallas kernels, shards(): pl.pallas_call(functools.partial(kernel, ngx, ngy), out_shape=(jax.ShapeD...  31.6 us
    pallas_call x1, Pallas kernels, shards(): pl.pallas_call(finish, out_shape=(jax.ShapeDtypeStruct(pressure.shape, F3...  1.34 us

profile of v4, /device:TPU:1, one launch (start us, length us, event | category | flops | bytes accessed | tf_op | source)
XLA Modules:
  0.0 33.6 jit_solution(11721912287367277575)
XLA Ops:
  0.6 31.6 %shard_map.104 = (f32[64,16,512]{2,1,0:T(8,128)S(1)}, f32[3,32,3072]{2,1,0:T(8,128)S(1)}, f32[48,256]{1,0:T(8,128)S(1)}, f32[48,256]{1,0:T(8,128)S(1)}, f32[32,1...) custom-call(f32[64,16,512]{2,1,0:T(8,128)} %p_hbm.1, f32[64,16,512]{2,1,0:T(8,128)} %d_hbm.1, ...), custom_call_target="tpu_custom_call" | custom-call | tf_op jit(solution)/shard_map/pallas_call | solution.py:548
  32.3 1.3 %shard_map.105 = (f32[64,16,512]{2,1,0:T(8,128)}, f32[3,3072]{1,0:T(4,128)}) custom-call(f32[64,16,512]{2,1,0:T(8,128)S(1)} %get-tuple-element.9.p_new, f32[3,32,3072]{2,1,0:T(8,128)S(1)} %get-tuple-element.10.ww, f32[48,256]{1,0:T(8,128)S(1)} %get-tuple-element.11.xs, f32[48,256]{1,0:T(8,128)S(1)} %get-tuple-element.12.occ, ...), custom_call_target="tpu_custom_call" | custom-call | tf_op jit(solution)/shard_map/pallas_call | solution.py:619
